TPU v7x, 1024 devices: a whole 4x8x16 slice. The times are simulated.
1024 devices in a mesh: gx: 4 (over y_lo), gy: 16 (over z), gz: 16 (over x, y_hi, core).
Axes of the slice: x: 4, y: 8 (y_hi: 2, y_lo: 4; y = y_hi * 4 + y_lo), z: 16, core: 2. Of those that a mesh axis runs over, the one named last changes fastest.
Arguments:
- positions: float32 [4, 16, 16, 3, 48], P('gx', 'gy', 'gz'), may hold values from 0 to 1
- species: int32 [4, 16, 16, 48], P('gx', 'gy', 'gz'), may hold values from 0 to 3
- neighbours: int32 [4, 16, 16, 48, 128], P('gx', 'gy', 'gz'), may hold values from 0 to 1295
- neigh_counts: int32 [4, 16, 16, 48], P('gx', 'gy', 'gz'), may hold values from 64 to 128
- embedding: bfloat16 [4, 128], replicated, may hold values from -6 to 6
- rbf_decay: float32 [16], replicated, may hold values from 0.2 to 5
- radial_weight: bfloat16 [2, 16, 128], replicated, may hold values from -1.5 to 1.5
- node_weight: bfloat16 [2, 128, 128], replicated, may hold values from -0.5 to 0.5
- readout: bfloat16 [128], replicated, may hold values from -0.5 to 0.5
- species_bias: float32 [4], replicated, may hold values from -4 to 4
Outputs:
- atom_energy: float32 [4, 16, 16, 48], P('gx', 'gy', 'gz')
- total_energy: float32 [], replicated
Inputs may be any that keep to these rules, and one draw needn't show every extreme that they name: `neighbours`: the offset code of an entry is 9 (dx + 1) + 3 (dy + 1) + (dz + 1) for a cell offset of -1, 0 or 1 along each dimension.
All inputs are finite; a program needn't handle non-finite values.
Results may differ from a plain program's by a relative error of at most 0.0028.
Values may be sent and summed in bfloat16 or wider, within the bound.
No kernel may reach another device: no remote copies, remote signals or barrier semaphores. Data moves between devices by JAX's collectives and lax.ppermute only.
A program may use at most 32 MiB of HBM per device.

v0:
```python
import functools

import jax
import jax.numpy as jnp
from jax import lax
from jax.sharding import Mesh
from jax.sharding import PartitionSpec as P

LAYERS = 2
GX_GY_GZ = ("gx", "gy", "gz_0", "gz_1", "gz_2")
GZ = ("gz_0", "gz_1", "gz_2")


def extended_2(block, sides, width):
    for axis, dim in sides:
        count = lax.axis_size(axis)
        forward = [(i, i + 1) for i in range(count - 1)]
        forward.append((count - 1, 0))
        backward = [(target, source) for source, target in forward]
        low = lax.ppermute(
            lax.slice_in_dim(block, block.shape[dim] - width, None, axis=dim), axis, forward
        )
        high = lax.ppermute(lax.slice_in_dim(block, 0, width, axis=dim), axis, backward)
        block = jnp.concatenate([low, block, high], axis=dim)
    return block


def by_axis(value, axes):
    return functools.reduce(lax.psum, axes, value)


def embed_atoms(species, embedding):
    kind_count = embedding.shape[0]
    one_hot = (species[..., None] == jnp.arange(kind_count, dtype=jnp.int32)).astype(jnp.bfloat16)
    embedded = jnp.dot(
        one_hot.reshape(-1, kind_count), embedding, preferred_element_type=jnp.float32
    )
    return embedded.astype(jnp.bfloat16).reshape(species.shape + (embedding.shape[1],))


def interaction(
    hidden_slab, place_slab, neighbour_row, count_row, rbf_decay, radial_weight, node_weight
):
    cell_count, slot_count, neighbour_count = neighbour_row.shape
    feature_width = hidden_slab.shape[-1]
    basis_count = rbf_decay.shape[0]
    slab_depth = cell_count + 2
    code_offset = neighbour_row // slot_count
    slot_index = neighbour_row % slot_count
    shift_x = code_offset // 9
    shift_y = code_offset // 3 % 3
    shift_z = code_offset % 3
    cell_column = lax.broadcasted_iota(jnp.int32, neighbour_row.shape, 0)
    cell_index = ((shift_x * 3 + shift_y) * slab_depth + cell_column + shift_z).reshape(-1)
    slot_flat = slot_index.reshape(-1)
    neighbour_feats = jnp.take(
        hidden_slab.reshape(-1, feature_width), cell_index * slot_count + slot_flat, axis=0
    )
    neighbour_feats = neighbour_feats.reshape(
        cell_count * slot_count, neighbour_count, feature_width
    )
    place_flat = place_slab.reshape(9 * slab_depth, 3, slot_count)
    far_place = place_flat[cell_index, :, slot_flat]
    centre = jnp.transpose(place_slab[1, 1, 1 : slab_depth - 1], (0, 2, 1))
    offsets_xyz = jnp.stack([shift_x - 1, shift_y - 1, shift_z - 1], axis=-1).astype(jnp.float32)
    displace = (
        far_place.reshape(cell_count, slot_count, neighbour_count, 3)
        + offsets_xyz
        - centre[:, :, None, :]
    )
    distance_sq = jnp.sum(displace * displace, axis=-1)
    radial_basis = jnp.exp(-distance_sq[..., None] * rbf_decay).astype(jnp.bfloat16)
    live_mask = lax.broadcasted_iota(jnp.int32, neighbour_row.shape, 2) < count_row[:, :, None]
    radial_basis = jnp.where(live_mask[..., None], radial_basis, jnp.bfloat16(0.0))
    radial_basis = radial_basis.reshape(cell_count * slot_count, neighbour_count, basis_count)
    collected = jnp.einsum(
        "anb,anf->abf", radial_basis, neighbour_feats, preferred_element_type=jnp.float32
    )
    message = jnp.sum(collected * radial_weight.astype(jnp.float32)[None], axis=1)
    inv_scale = lax.rsqrt(jnp.mean(message * message, axis=-1, keepdims=True) + 1e-05)
    normed = (message * inv_scale).astype(jnp.bfloat16)
    update = jax.nn.silu(jnp.dot(normed, node_weight, preferred_element_type=jnp.float32))
    own_rows = hidden_slab[1, 1, 1 : slab_depth - 1].reshape(-1, feature_width).astype(jnp.float32)
    return (own_rows + update).astype(jnp.bfloat16).reshape(cell_count, slot_count, feature_width)


def run_layer(
    hidden_pad, place_pad, neighbours, neigh_counts, rbf_decay, radial_weight, node_weight
):
    span_x = neighbours.shape[0]
    span_y = neighbours.shape[1]

    def one_row(row_index):
        row_x = row_index // span_y
        row_y = row_index % span_y
        return interaction(
            hidden_pad,
            place_pad,
            neighbours[row_x, row_y],
            neigh_counts[row_x, row_y],
            rbf_decay,
            radial_weight,
            node_weight,
        )

    row_results = lax.map(one_row, jnp.arange(span_x * span_y, dtype=jnp.int32))
    return row_results.reshape((span_x, span_y) + row_results.shape[1:])


def atom_energies(hidden, species, readout, species_bias):
    per_atom = jnp.sum(hidden.astype(jnp.float32) * readout.astype(jnp.float32), axis=-1)
    one_hot = (species[..., None] == jnp.arange(species_bias.shape[0], dtype=jnp.int32)).astype(
        jnp.float32
    )
    return per_atom + jnp.sum(one_hot * species_bias, axis=-1)


def body(
    positions,
    species,
    neighbours,
    neigh_counts,
    embedding,
    rbf_decay,
    radial_weight,
    node_weight,
    readout,
    species_bias,
):
    records = jnp.concatenate([positions, species.astype(jnp.float32)[:, :, :, None, :]], axis=3)
    extended = extended_2(records, (("gx", 0), ("gy", 1), (GZ, 2)), 1)
    place_pad = extended[:, :, :, 0:3]
    hidden_pad = embed_atoms(extended[:, :, :, 3].astype(jnp.int32), embedding)
    hidden = None
    for layer_index in range(LAYERS):
        if layer_index > 0:
            hidden_pad = extended_2(hidden, (("gx", 0), ("gy", 1), (GZ, 2)), 1)
        hidden = run_layer(
            hidden_pad,
            place_pad,
            neighbours,
            neigh_counts,
            rbf_decay,
            radial_weight[layer_index],
            node_weight[layer_index],
        )
    energy = atom_energies(hidden, species, readout, species_bias)
    total = by_axis(jnp.sum(energy), GX_GY_GZ)
    return (energy, total)


def solution(mesh):
    finer = Mesh(
        mesh.devices.reshape(mesh.shape["gx"], mesh.shape["gy"], 4, 2, 2),
        ("gx", "gy", "gz_0", "gz_1", "gz_2"),
    )
    in_specs = (
        P("gx", "gy", GZ, None, None),
        P("gx", "gy", GZ, None),
        P("gx", "gy", GZ, None, None),
        P("gx", "gy", GZ, None),
        P(),
        P(),
        P(),
        P(),
        P(),
        P(),
    )
    out_specs = (P("gx", "gy", GZ, None), P())
    return jax.shard_map(body, mesh=finer, in_specs=in_specs, out_specs=out_specs, check_vma=False)
```

profile of v0, /device:TPU:1, one launch (start us, length us, event | category | flops | bytes accessed | tf_op | source)
XLA Modules:
  0.0 263.9 jit_solution(11893859287888244697)
XLA Ops:
  0.6 0.7 convert_bitcast_fusion
  1.3 0.7 pad_maximum_fusion.6
  2.0 4.0 %collective-permute-start = (f32[1,1,1,4,48]{4,2,3,1,0:T(1,128)S(1)}, f32[1,1,1,4,48]{4,2,3,1,0:T(1,128)S(1)}, u32[]{:S(2)}, u32[]{:S(2)}) collective-permute-start(f32[1,1,1,4,48]{4,2,3,1,0:T(1,128)S(1)} %pad_maximum_fusion.6), channel_id=1, source_target_pairs={{0,256},{256,512},{512,768},{768,0},{1,257},{257,513},{513,769},{7... | collective-permute-start | bytes 2312 | tf_op jit(solution)/shard_map/ppermute | solution.py:20
  6.0 3.9 %collective-permute-start.1 = (f32[1,1,1,4,48]{4,2,3,1,0:T(1,128)S(1)}, f32[1,1,1,4,48]{4,2,3,1,0:T(1,128)S(1)}, u32[]{:S(2)}, u32[]{:S(2)}) collective-permute-start(f32[1,1,1,4,48]{4,2,3,1,0:T(1,128)S(1)} %pad_maximum_fusion.6), channel_id=1, source_target_pairs={{256,0},{512,256},{768,512},{0,768},{257,1},{513,257},{769,513},{1... | collective-permute-start | bytes 2312 | tf_op jit(solution)/shard_map/ppermute | solution.py:23
  10.0 0.8 broadcast_divide_fusion
  10.7 0.8 compare_and_fusion
  11.6 0.2 broadcast_add_fusion.2
  11.8 0.3 broadcast_add_fusion.1
  12.1 0.3 fusion.34
  12.4 0.7 pad_maximum_fusion.5
  13.1 4.0 %collective-permute-start.2 = (f32[3,1,1,4,48]{4,2,3,1,0:T(1,128)S(1)}, f32[3,1,1,4,48]{4,2,3,1,0:T(1,128)S(1)}, u32[]{:S(2)}, u32[]{:S(2)}) collective-permute-start(f32[3,1,1,4,48]{4,2,3,1,0:T(1,128)S(1)} %pad_maximum_fusion.5), channel_id=1, source_target_pairs={{0,16},{16,32},{32,48},{48,64},{64,80},{80,96},{96,112},{112,128},... | collective-permute-start | bytes 6920 | tf_op jit(solution)/shard_map/ppermute | solution.py:20
  17.1 15.9 %collective-permute-start.3 = (f32[3,1,1,4,48]{4,2,3,1,0:T(1,128)S(1)}, f32[3,1,1,4,48]{4,2,3,1,0:T(1,128)S(1)}, u32[]{:S(2)}, u32[]{:S(2)}) collective-permute-start(f32[3,1,1,4,48]{4,2,3,1,0:T(1,128)S(1)} %pad_maximum_fusion.5), channel_id=1, source_target_pairs={{16,0},{32,16},{48,32},{64,48},{80,64},{96,80},{112,96},{128,112},... | collective-permute-start | bytes 6920 | tf_op jit(solution)/shard_map/ppermute | solution.py:23
  32.9 0.7 bitcast_convert_fusion
  33.7 0.7 pad_maximum_fusion.4
  34.4 9.4 %collective-permute-start.4 = (f32[3,3,1,4,48]{4,2,3,1,0:T(1,128)S(1)}, f32[3,3,1,4,48]{4,2,3,1,0:T(1,128)S(1)}, u32[]{:S(2)}, u32[]{:S(2)}) collective-permute-start(f32[3,3,1,4,48]{4,2,3,1,0:T(1,128)S(1)} %pad_maximum_fusion.4), channel_id=1, source_target_pairs={{0,1},{1,2},{2,3},{3,4},{4,5},{5,6},{6,7},{7,8},{8,9},{9,10},{10,1... | collective-permute-start | bytes 20744 | tf_op jit(solution)/shard_map/ppermute | solution.py:20
  43.8 1.9 collective-permute-start.5
  45.7 0.7 iota_compare_fusion.2
  46.4 0.7 copy.26
  47.1 5.6 %collective-permute-done.5 = f32[3,3,1,4,48]{4,2,3,1,0:T(1,128)S(1)} collective-permute-done((f32[3,3,1,4,48]{4,2,3,1,0:T(1,128)S(1)}, f32[3,3,1,4,48]{4,2,3,1,0:T(1,128)S(1)}, u32[]{:S(2)}, u32[]{:S(2)}) %collective-permute-start.5) | collective-permute-done | bytes 6944 | tf_op jit(solution)/shard_map/ppermute | solution.py:23
  52.7 0.7 pad_maximum_fusion.2
  53.5 0.3 copy.19
  53.8 66.4 %gather_fusion = f32[6144,3]{1,0:T(8,128)} fusion(f32[27,3,48]{1,2,0:T(8,128)S(1)} %bitcast.86, s32[6144]{0:T(1024)S(1)} %bitcast.89), kind=kCustom, calls=%fused_computation.2 | custom fusion | bytes 196608 | tf_op jit(solution)/shard_map/while/body/eval_jaxpr/gather | solution.py:63
  120.2 2.4 copy.20
  122.8 0.4 convolution_convert_fusion
  123.1 18.1 %gather_fusion.1 = bf16[6144,128]{1,0:T(8,128)(2,1)S(1)} fusion(bf16[1296,128]{1,0:T(8,128)(2,1)S(1)} %convolution_convert_fusion, s32[6144]{0:T(1024)S(1)} %broadcast_clamp_fusion), kind=kCustom, calls=%fused_computation.clone | custom fusion | bytes 3170304 | tf_op jit(solution)/shard_map/while/body/eval_jaxpr/jit(_take)/gather | solution.py:56
  141.3 3.2 %broadcast_select_fusion.1 = bf16[6144,128]{1,0:T(8,128)(2,1)S(1)} fusion(bf16[6144,128]{1,0:T(8,128)(2,1)S(1)} %gather_fusion.1, pred[6144]{0:T(1024)(128)(4,1)S(1)} %get-tuple-element.48), kind=kLoop, calls=%fused_computation.5 | loop fusion | flops 786432 | bytes 3151872 | tf_op jit(solution)/shard_map/while/body/eval_jaxpr/jit(_take)/select_n | solution.py:56
  144.5 0.6 fusion
  145.3 0.2 fusion.37
  145.5 1.9 collective-permute-start.6
  147.5 5.2 %collective-permute-start.7 = (bf16[1,1,1,48,128]{4,3,2,1,0:T(8,128)(2,1)S(1)}, bf16[1,1,1,48,128]{4,3,2,1,0:T(8,128)(2,1)S(1)}, u32[]{:S(2)}, u32[]{:S(2)}) collective-permute-start(bf16[1,1,1,48,128]{4,3,2,1,0:T(8,128)(2,1)S(1)} %bitcast.96), channel_id=1, source_target_pairs={{256,0},{512,256},{768,512},{0,768},{257,1},{513,257},{769,513},{1... | collective-permute-start | bytes 36872 | tf_op jit(solution)/shard_map/ppermute | solution.py:23
  152.6 0.8 collective-permute-done.7
  153.4 1.9 collective-permute-start.8
  155.4 5.1 %collective-permute-start.9 = (bf16[3,1,1,48,128]{4,3,2,1,0:T(8,128)(2,1)S(1)}, bf16[3,1,1,48,128]{4,3,2,1,0:T(8,128)(2,1)S(1)}, u32[]{:S(2)}, u32[]{:S(2)}) collective-permute-start(bf16[3,1,1,48,128]{4,3,2,1,0:T(8,128)(2,1)S(1)} %pad_maximum_fusion.3), channel_id=1, source_target_pairs={{16,0},{32,16},{48,32},{64,48},{80,64},{96,80},{112,96},{128,112},... | collective-permute-start | bytes 110600 | tf_op jit(solution)/shard_map/ppermute | solution.py:23
  160.5 1.0 collective-permute-done.9
  161.5 4.1 %collective-permute-start.10 = (bf16[3,3,1,48,128]{4,3,2,1,0:T(8,128)(2,1)S(1)}, bf16[3,3,1,48,128]{4,3,2,1,0:T(8,128)(2,1)S(1)}, u32[]{:S(2)}, u32[]{:S(2)}) collective-permute-start(bf16[3,3,1,48,128]{4,3,2,1,0:T(8,128)(2,1)S(1)} %pad_maximum_fusion.1), channel_id=1, source_target_pairs={{0,1},{1,2},{2,3},{3,4},{4,5},{5,6},{6,7},{7,8},{8,9},{9,10},{10,1... | collective-permute-start | bytes 331784 | tf_op jit(solution)/shard_map/ppermute | solution.py:20
  165.6 1.9 collective-permute-start.11
  167.7 0.1 collective-permute-done.10
  167.8 7.9 %collective-permute-done.11 = bf16[3,3,1,48,128]{4,3,2,1,0:T(8,128)(2,1)S(1)} collective-permute-done((bf16[3,3,1,48,128]{4,3,2,1,0:T(8,128)(2,1)S(1)}, bf16[3,3,1,48,128]{4,3,2,1,0:T(8,128)(2,1)S(1)}, u32[]{:S(2)}, u32[]{:S(2)}) %collective-permute-start.11) | collective-permute-done | bytes 110624 | tf_op jit(solution)/shard_map/ppermute | solution.py:23
  175.7 18.1 %gather_fusion.2 = bf16[6144,128]{1,0:T(8,128)(2,1)S(1)} fusion(bf16[1296,128]{1,0:T(8,128)(2,1)S(1)} %bitcast.88, s32[6144]{0:T(1024)S(1)} %broadcast_clamp_fusion), kind=kCustom, calls=%fused_computation.1.clone | custom fusion | bytes 3170304 | tf_op jit(solution)/shard_map/while/body/eval_jaxpr/jit(_take)/gather | solution.py:56
  193.9 3.2 %broadcast_select_fusion = bf16[6144,128]{1,0:T(8,128)(2,1)S(1)} fusion(bf16[6144,128]{1,0:T(8,128)(2,1)S(1)} %gather_fusion.2, pred[6144]{0:T(1024)(128)(4,1)S(1)} %get-tuple-element.48), kind=kLoop, calls=%fused_computation.4 | loop fusion | flops 786432 | bytes 3151872 | tf_op jit(solution)/shard_map/while/body/eval_jaxpr/jit(_take)/select_n | solution.py:56
  197.1 0.6 fusion.1
  197.8 0.3 multiply_reduce_fusion
  198.1 1.1 add_reduce_fusion
  199.2 12.0 %psum.35 = f32[]{:T(128)} all-reduce(f32[]{:T(128)} %get-tuple-element.66), channel_id=1, replica_groups=mesh['gx'=4,'gy'=16,'gz_0'=4,'gz_1'=2,'gz_2'=2] {'gx'}, use_global_device_ids=true, to_apply=%region_8.10 | all-reduce | flops 1 | bytes 8 | tf_op jit(solution)/shard_map/psum | solution.py:29
  211.2 24.2 %psum.36 = f32[]{:T(128)} all-reduce(f32[]{:T(128)} %psum.35), channel_id=1, replica_groups=mesh['gx'=4,'gy'=16,'gz_0'=4,'gz_1'=2,'gz_2'=2] {'gy'}, use_global_device_ids=true, to_apply=%region_9.11 | all-reduce | flops 1 | bytes 8 | tf_op jit(solution)/shard_map/psum | solution.py:29
  235.4 8.2 %psum.37 = f32[]{:T(128)} all-reduce(f32[]{:T(128)} %psum.36), channel_id=1, replica_groups=mesh['gx'=4,'gy'=16,'gz_0'=4,'gz_1'=2,'gz_2'=2] {'gz_0'}, use_global_device_ids=true, to_apply=%region_10.12 | all-reduce | flops 1 | bytes 8 | tf_op jit(solution)/shard_map/psum | solution.py:29
  243.6 8.3 %psum.38 = f32[]{:T(128)} all-reduce(f32[]{:T(128)} %psum.37), channel_id=1, replica_groups=mesh['gx'=4,'gy'=16,'gz_0'=4,'gz_1'=2,'gz_2'=2] {'gz_1'}, use_global_device_ids=true, to_apply=%region_11.13 | all-reduce | flops 1 | bytes 8 | tf_op jit(solution)/shard_map/psum | solution.py:29
  251.9 12.0 %psum.39 = f32[]{:T(128)} all-reduce(f32[]{:T(128)} %psum.38), channel_id=1, replica_groups=mesh['gx'=4,'gy'=16,'gz_0'=4,'gz_1'=2,'gz_2'=2] {'gz_2'}, use_global_device_ids=true, to_apply=%region_12.14 | all-reduce | flops 1 | bytes 8 | tf_op jit(solution)/shard_map/psum | solution.py:29
  (34 shorter events, 0.7 us)
Async XLA Ops:
  0.6 122.1 %copy-start = (bf16[4,128]{1,0:T(4,128)(2,1)S(1)}, bf16[4,128]{1,0:T(4,128)(2,1)}, u32[]{:S(2)}) copy-start(bf16[4,128]{1,0:T(4,128)(2,1)} %param.16) | copy-start | bytes 3076
  2.0 10.4 %collective-permute-start = (f32[1,1,1,4,48]{4,2,3,1,0:T(1,128)S(1)}, f32[1,1,1,4,48]{4,2,3,1,0:T(1,128)S(1)}, u32[]{:S(2)}, u32[]{:S(2)}) collective-permute-start(f32[1,1,1,4,48]{4,2,3,1,0:T(1,128)S(1)} %pad_maximum_fusion.6), channel_id=1, source_target_pairs={{0,256},{256,512},{512,768},{768,0},{1,257},{257,513},{513,769},{7... | collective-permute-start | bytes 2312 | tf_op jit(solution)/shard_map/ppermute | solution.py:20
  6.0 6.4 %collective-permute-start.1 = (f32[1,1,1,4,48]{4,2,3,1,0:T(1,128)S(1)}, f32[1,1,1,4,48]{4,2,3,1,0:T(1,128)S(1)}, u32[]{:S(2)}, u32[]{:S(2)}) collective-permute-start(f32[1,1,1,4,48]{4,2,3,1,0:T(1,128)S(1)} %pad_maximum_fusion.6), channel_id=1, source_target_pairs={{256,0},{512,256},{768,512},{0,768},{257,1},{513,257},{769,513},{1... | collective-permute-start | bytes 2312 | tf_op jit(solution)/shard_map/ppermute | solution.py:23
  13.1 20.6 %collective-permute-start.2 = (f32[3,1,1,4,48]{4,2,3,1,0:T(1,128)S(1)}, f32[3,1,1,4,48]{4,2,3,1,0:T(1,128)S(1)}, u32[]{:S(2)}, u32[]{:S(2)}) collective-permute-start(f32[3,1,1,4,48]{4,2,3,1,0:T(1,128)S(1)} %pad_maximum_fusion.5), channel_id=1, source_target_pairs={{0,16},{16,32},{32,48},{48,64},{64,80},{80,96},{96,112},{112,128},... | collective-permute-start | bytes 6920 | tf_op jit(solution)/shard_map/ppermute | solution.py:20
  17.1 16.6 %collective-permute-start.3 = (f32[3,1,1,4,48]{4,2,3,1,0:T(1,128)S(1)}, f32[3,1,1,4,48]{4,2,3,1,0:T(1,128)S(1)}, u32[]{:S(2)}, u32[]{:S(2)}) collective-permute-start(f32[3,1,1,4,48]{4,2,3,1,0:T(1,128)S(1)} %pad_maximum_fusion.5), channel_id=1, source_target_pairs={{16,0},{32,16},{48,32},{64,48},{80,64},{96,80},{112,96},{128,112},... | collective-permute-start | bytes 6920 | tf_op jit(solution)/shard_map/ppermute | solution.py:23
  34.4 12.7 %collective-permute-start.4 = (f32[3,3,1,4,48]{4,2,3,1,0:T(1,128)S(1)}, f32[3,3,1,4,48]{4,2,3,1,0:T(1,128)S(1)}, u32[]{:S(2)}, u32[]{:S(2)}) collective-permute-start(f32[3,3,1,4,48]{4,2,3,1,0:T(1,128)S(1)} %pad_maximum_fusion.4), channel_id=1, source_target_pairs={{0,1},{1,2},{2,3},{3,4},{4,5},{5,6},{6,7},{7,8},{8,9},{9,10},{10,1... | collective-permute-start | bytes 20744 | tf_op jit(solution)/shard_map/ppermute | solution.py:20
  43.8 9.0 %collective-permute-start.5 = (f32[3,3,1,4,48]{4,2,3,1,0:T(1,128)S(1)}, f32[3,3,1,4,48]{4,2,3,1,0:T(1,128)S(1)}, u32[]{:S(2)}, u32[]{:S(2)}) collective-permute-start(f32[3,3,1,4,48]{4,2,3,1,0:T(1,128)S(1)} %pad_maximum_fusion.4), channel_id=1, source_target_pairs={{1,0},{2,1},{3,2},{4,3},{5,4},{6,5},{7,6},{8,7},{9,8},{10,9},{11,1... | collective-permute-start | bytes 20744 | tf_op jit(solution)/shard_map/ppermute | solution.py:23
  141.2 3.3 %copy-start.1 = (f32[16]{0:T(128)S(1)}, f32[16]{0:T(128)}, u32[]{:S(2)}) copy-start(f32[16]{0:T(128)} %param.17) | copy-start | bytes 196
  144.5 0.8 copy-start.2
  144.5 16.0 %copy-start.3 = (bf16[128]{0:T(256)(128)(2,1)S(1)}, bf16[128]{0:T(256)(128)(2,1)}, u32[]{:S(2)}) copy-start(bf16[128]{0:T(256)(128)(2,1)} %param.20) | copy-start | bytes 772
  144.5 23.1 %copy-start.4 = (s32[1,1,1,48]{3,2,1,0:T(1,128)S(1)}, s32[1,1,1,48]{3,2,1,0:T(1,128)}, u32[]{:S(2)}) copy-start(s32[1,1,1,48]{3,2,1,0:T(1,128)} %param.13) | copy-start | bytes 580
  144.5 23.1 %copy-start.5 = (f32[4]{0:T(128)S(1)}, f32[4]{0:T(128)}, u32[]{:S(2)}) copy-start(f32[4]{0:T(128)} %param.21) | copy-start | bytes 52
  145.5 7.1 %collective-permute-start.6 = (bf16[1,1,1,48,128]{4,3,2,1,0:T(8,128)(2,1)S(1)}, bf16[1,1,1,48,128]{4,3,2,1,0:T(8,128)(2,1)S(1)}, u32[]{:S(2)}, u32[]{:S(2)}) collective-permute-start(bf16[1,1,1,48,128]{4,3,2,1,0:T(8,128)(2,1)S(1)} %bitcast.95), channel_id=1, source_target_pairs={{0,256},{256,512},{512,768},{768,0},{1,257},{257,513},{513,769},{7... | collective-permute-start | bytes 36872 | tf_op jit(solution)/shard_map/ppermute | solution.py:20
  147.5 6.0 %collective-permute-start.7 = (bf16[1,1,1,48,128]{4,3,2,1,0:T(8,128)(2,1)S(1)}, bf16[1,1,1,48,128]{4,3,2,1,0:T(8,128)(2,1)S(1)}, u32[]{:S(2)}, u32[]{:S(2)}) collective-permute-start(bf16[1,1,1,48,128]{4,3,2,1,0:T(8,128)(2,1)S(1)} %bitcast.96), channel_id=1, source_target_pairs={{256,0},{512,256},{768,512},{0,768},{257,1},{513,257},{769,513},{1... | collective-permute-start | bytes 36872 | tf_op jit(solution)/shard_map/ppermute | solution.py:23
  153.4 7.1 %collective-permute-start.8 = (bf16[3,1,1,48,128]{4,3,2,1,0:T(8,128)(2,1)S(1)}, bf16[3,1,1,48,128]{4,3,2,1,0:T(8,128)(2,1)S(1)}, u32[]{:S(2)}, u32[]{:S(2)}) collective-permute-start(bf16[3,1,1,48,128]{4,3,2,1,0:T(8,128)(2,1)S(1)} %pad_maximum_fusion.3), channel_id=1, source_target_pairs={{0,16},{16,32},{32,48},{48,64},{64,80},{80,96},{96,112},{112,128},... | collective-permute-start | bytes 110600 | tf_op jit(solution)/shard_map/ppermute | solution.py:20
  155.4 6.2 %collective-permute-start.9 = (bf16[3,1,1,48,128]{4,3,2,1,0:T(8,128)(2,1)S(1)}, bf16[3,1,1,48,128]{4,3,2,1,0:T(8,128)(2,1)S(1)}, u32[]{:S(2)}, u32[]{:S(2)}) collective-permute-start(bf16[3,1,1,48,128]{4,3,2,1,0:T(8,128)(2,1)S(1)} %pad_maximum_fusion.3), channel_id=1, source_target_pairs={{16,0},{32,16},{48,32},{64,48},{80,64},{96,80},{112,96},{128,112},... | collective-permute-start | bytes 110600 | tf_op jit(solution)/shard_map/ppermute | solution.py:23
  161.5 6.2 %collective-permute-start.10 = (bf16[3,3,1,48,128]{4,3,2,1,0:T(8,128)(2,1)S(1)}, bf16[3,3,1,48,128]{4,3,2,1,0:T(8,128)(2,1)S(1)}, u32[]{:S(2)}, u32[]{:S(2)}) collective-permute-start(bf16[3,3,1,48,128]{4,3,2,1,0:T(8,128)(2,1)S(1)} %pad_maximum_fusion.1), channel_id=1, source_target_pairs={{0,1},{1,2},{2,3},{3,4},{4,5},{5,6},{6,7},{7,8},{8,9},{9,10},{10,1... | collective-permute-start | bytes 331784 | tf_op jit(solution)/shard_map/ppermute | solution.py:20
  165.6 10.1 %collective-permute-start.11 = (bf16[3,3,1,48,128]{4,3,2,1,0:T(8,128)(2,1)S(1)}, bf16[3,3,1,48,128]{4,3,2,1,0:T(8,128)(2,1)S(1)}, u32[]{:S(2)}, u32[]{:S(2)}) collective-permute-start(bf16[3,3,1,48,128]{4,3,2,1,0:T(8,128)(2,1)S(1)} %pad_maximum_fusion.1), channel_id=1, source_target_pairs={{1,0},{2,1},{3,2},{4,3},{5,4},{6,5},{7,6},{8,7},{9,8},{10,9},{11,1... | collective-permute-start | bytes 331784 | tf_op jit(solution)/shard_map/ppermute | solution.py:23
where the time goes:
time: 265 us; the launch traced here: 264 us
  local copies, waits for them, and re-layouts  106 us (40%)
  blocking collectives  64.6 us (24%)
  starting transfers between devices  59.2 us (22%)
  waiting for transfers between devices  15.5 us (6%)
  other arithmetic  15.3 us (6%)
    gather x2, local copies, waits for them, and re-layouts, interaction(): far_place = place_flat[cell_index, :, slot_flat]  68.7 us
    psum x5, blocking collectives, by_axis(): return functools.reduce(lax.psum, axes, value)  64.6 us
    gather x2, local copies, waits for them, and re-layouts, interaction(): jnp.take(hidden_slab.reshape(-1, feature_width), cell_index * slot_count...  36.2 us
    ppermute x6, starting transfers between devices, extended_2(): lax.ppermute(lax.slice_in_dim(block, 0, width, axis=dim), axis, backward)  33.9 us
    ppermute x6, starting transfers between devices, extended_2(): lax.ppermute(lax.slice_in_dim(block, block.shape[dim] - width, None, axis...  25.3 us
    ppermute x6, waiting for transfers between devices, extended_2(): lax.ppermute(lax.slice_in_dim(block, 0, width, axis=dim), axis, backward)  15.4 us
    select_n x2, other arithmetic, interaction(): jnp.take(hidden_slab.reshape(-1, feature_width), cell_index * slot_count...  6.42 us
  transfers between devices with their start and end apart: 12, of which 5 were waited for; matrix products, arithmetic and copies ran while one was open for 2% of the time, Pallas kernels for 0%

commit v1 on v0

v1 whole, which is shorter than its diff:
```python
import jax
import jax.numpy as jnp
from jax import lax
from jax.experimental import pallas as pl
from jax.experimental.pallas import tpu as pltpu
from jax.sharding import PartitionSpec as P

F = 128
NB = 128
NRBF = 16
SLOTS = 48
LAYERS = 2
PLANE = 9 * SLOTS
LANES = 512
TILES = 3 * LANES // 128
AXES = ("gx", "gy", "gz")
SMALL = pltpu.CompilerParams(vmem_limit_bytes=16 * 1024 * 1024)


def kept(array):
    return pltpu.with_memory_space_constraint(array, pltpu.VMEM)


def count_kernel(neighbours, counts, out, high, low, table):
    code = neighbours[...]
    offset = (code * 1366) >> 16
    slot = code - offset * SLOTS
    across = (offset * 171) >> 9
    depth = (across * 171) >> 9
    column = (across - depth * 3) * 3 + depth
    place = (offset - across * 3) * LANES + column * SLOTS + slot
    high[...] = place >> 7
    low[...] = place & 127
    lane = lax.broadcasted_iota(jnp.int32, (1, NB), 1)
    tile_of = lax.broadcasted_iota(jnp.int32, (16, NB), 0)
    lane_of = lax.broadcasted_iota(jnp.int32, (128, NB), 0)
    for atom in range(SLOTS):
        tile = jnp.where(lane < counts[atom], high[atom : atom + 1], -1)
        left = jnp.where(tile == tile_of, 1.0, 0.0).astype(jnp.bfloat16)
        right = jnp.where(low[atom : atom + 1] == lane_of, 1.0, 0.0).astype(jnp.bfloat16)
        table[atom * 16 : atom * 16 + 16] = lax.dot_general(
            left, right, (((1,), (1,)), ((), ())), preferred_element_type=jnp.float32
        )
    for tile in range(TILES):
        out[:, tile * 128 : tile * 128 + 128] = table[pl.ds(tile, SLOTS, stride=16), :].astype(
            jnp.bfloat16
        )


def count_table(neighbours, counts):
    return pl.pallas_call(
        count_kernel,
        out_shape=pltpu.VMEM((SLOTS, 3 * LANES), jnp.bfloat16),
        in_specs=[
            pl.BlockSpec(memory_space=pltpu.VMEM),
            pl.BlockSpec(memory_space=pltpu.SMEM),
        ],
        out_specs=pl.BlockSpec(memory_space=pltpu.VMEM),
        scratch_shapes=[
            pltpu.VMEM((SLOTS, NB), jnp.int32),
            pltpu.VMEM((SLOTS, NB), jnp.int32),
            pltpu.VMEM((SLOTS * 16, 128), jnp.float32),
        ],
        compiler_params=SMALL,
        name="count_table",
    )(neighbours, counts)


def node_update(edges, tables, radial, weight):
    message = jnp.zeros((SLOTS, F), jnp.float32)
    gathered = None
    for z in range(3):
        part = jnp.dot(
            edges[:, z * LANES : z * LANES + PLANE],
            tables[z],
            preferred_element_type=jnp.float32,
        )
        gathered = part if gathered is None else gathered + part
    weights = radial[...].astype(jnp.float32)
    for b in range(NRBF):
        message = message + gathered[b * SLOTS : (b + 1) * SLOTS] * weights[b : b + 1]
    scale = lax.rsqrt(jnp.mean(message * message, axis=1, keepdims=True) + 1e-05)
    normed = (message * scale).astype(jnp.bfloat16)
    moved = jnp.dot(normed, weight[...], preferred_element_type=jnp.float32)
    own = tables[1][4 * SLOTS : 5 * SLOTS].astype(jnp.float32)
    return (own + moved / (1.0 + jnp.exp(-moved))).astype(jnp.bfloat16)


def first_kernel(
    below, middle, above, counts, decay, embedding, radial, weight, edges, hidden
):
    kinds = embedding[...]
    kind_of = lax.broadcasted_iota(jnp.int32, (8, LANES), 0).astype(jnp.float32)
    cell = lax.broadcasted_iota(jnp.int32, (4, LANES), 1) // SLOTS
    part_of = lax.broadcasted_iota(jnp.int32, (4, LANES), 0)
    centre = jnp.transpose(middle[4])
    tables = []
    for z, records in enumerate((below, middle, above)):
        pieces = [records[c] for c in range(9)]
        pieces.append(jnp.zeros((4, LANES - PLANE), jnp.float32))
        rows = jnp.concatenate(pieces, axis=1)
        shift = jnp.where(part_of == 0, cell % 3 - 1, jnp.where(part_of == 1, cell // 3 - 1, z - 1))
        moved = rows + shift.astype(jnp.float32)
        squared = None
        for d in range(3):
            away = moved[d : d + 1] - centre[:, d : d + 1]
            squared = away * away if squared is None else squared + away * away
        times = counts[:, z * LANES : (z + 1) * LANES]
        for b in range(NRBF):
            basis = jnp.exp(squared * (-decay[b])).astype(jnp.bfloat16)
            edges[b * SLOTS : (b + 1) * SLOTS, z * LANES : (z + 1) * LANES] = basis * times
        one_hot = jnp.where(rows[3:4] == kind_of, 1.0, 0.0)
        one_hot = jnp.transpose(one_hot).astype(jnp.bfloat16)
        table = jnp.dot(one_hot, kinds, preferred_element_type=jnp.float32)
        tables.append(table[:PLANE].astype(jnp.bfloat16))
    hidden[...] = node_update(edges, tables, radial, weight)


def first_layer(records, counts, decay, embedding, radial, weight):
    vmem = pl.BlockSpec(memory_space=pltpu.VMEM)
    smem = pl.BlockSpec(memory_space=pltpu.SMEM)
    return pl.pallas_call(
        first_kernel,
        out_shape=(
            pltpu.VMEM((NRBF * SLOTS, 3 * LANES), jnp.bfloat16),
            pltpu.VMEM((SLOTS, F), jnp.bfloat16),
        ),
        in_specs=[vmem, vmem, vmem, vmem, smem, vmem, vmem, vmem],
        out_specs=(vmem, vmem),
        compiler_params=SMALL,
        name="first_layer",
    )(*map(kept, records), kept(counts), decay, embedding, radial, weight)


def second_kernel(
    edges, below, middle, above, radial, weight, readout, species, bias, energy, total
):
    tables = [below[...], middle[...], above[...]]
    hidden = node_update(edges, tables, radial, weight)
    terms = hidden.astype(jnp.float32) * readout[...].astype(jnp.float32)
    per_atom = jnp.sum(jnp.transpose(terms), axis=0, keepdims=True)
    kind = species[...]
    offset = jnp.zeros((1, SLOTS), jnp.float32)
    for k in range(4):
        offset = offset + jnp.where(kind == k, bias[k], 0.0)
    result = per_atom + offset
    energy[...] = result
    total[...] = jnp.broadcast_to(jnp.sum(result, axis=1, keepdims=True), (1, 128))


def second_layer(edges, tables, radial, weight, readout, species, bias):
    vmem = pl.BlockSpec(memory_space=pltpu.VMEM)
    smem = pl.BlockSpec(memory_space=pltpu.SMEM)
    return pl.pallas_call(
        second_kernel,
        out_shape=(
            jax.ShapeDtypeStruct((1, SLOTS), jnp.float32),
            jax.ShapeDtypeStruct((1, 128), jnp.float32),
        ),
        in_specs=[vmem, vmem, vmem, vmem, vmem, vmem, vmem, vmem, smem],
        out_specs=(vmem, vmem),
        compiler_params=SMALL,
        name="second_layer",
    )(kept(edges), *map(kept, tables), radial, weight, readout, species, bias)


def both_ways(block, axis):
    count = lax.axis_size(axis)
    forward = [(i, (i + 1) % count) for i in range(count)]
    backward = [(target, source) for source, target in forward]
    return lax.ppermute(block, axis, forward), block, lax.ppermute(block, axis, backward)


def halo(block):
    row = jnp.concatenate(both_ways(block[None], "gx"), axis=0)
    sheet = jnp.concatenate(both_ways(row[None], "gy"), axis=0)
    return both_ways(sheet, "gz")


def summed(row):
    for axis in AXES:
        copies = jnp.broadcast_to(row[None], (lax.axis_size(axis),) + row.shape)
        row = jnp.sum(lax.all_to_all(copies, axis, 0, 0), axis=0)
    return row


def body(
    positions,
    species,
    neighbours,
    neigh_counts,
    embedding,
    rbf_decay,
    radial_weight,
    node_weight,
    readout,
    species_bias,
):
    kinds = species.reshape(1, SLOTS)
    records = jnp.concatenate([positions.reshape(3, SLOTS), kinds.astype(jnp.float32)], axis=0)
    counts = count_table(neighbours.reshape(SLOTS, NB), neigh_counts.reshape(SLOTS))
    places = [part.reshape(9, 4, SLOTS) for part in halo(records)]
    kinds_table = jnp.pad(embedding, ((0, 4), (0, 0)))
    edges, hidden = first_layer(
        places, counts, rbf_decay, kinds_table, radial_weight[0], node_weight[0]
    )
    tables = [part.reshape(PLANE, F) for part in halo(hidden)]
    energy, total = second_layer(
        edges, tables, radial_weight[1], node_weight[1], readout.reshape(1, F), kinds, species_bias
    )
    return energy.reshape(1, 1, 1, SLOTS), summed(total)[0, 0]


def solution(mesh):
    split = P("gx", "gy", "gz")
    in_specs = (split, split, split, split, P(), P(), P(), P(), P(), P())
    return jax.shard_map(
        body, mesh=mesh, in_specs=in_specs, out_specs=(split, P()), check_vma=False
    )
```

time: 265 us -> 133 us (0.50)
  local copies, waits for them, and re-layouts: 106 us -> 6.88 us
  blocking collectives: 64.6 us -> 43 us
  other arithmetic: 15.3 us -> 1.27 us
  Pallas kernels: 0 us -> 5.76 us
    gather x4 -> x0, local copies, waits for them, and re-layouts: 105 us -> none  [the longest x2 68.7 us: interaction(): far_place = place_flat[cell_index, :, slot_flat]]
    psum x5 -> x0, blocking collectives: 64.6 us -> none  [by_axis(): return functools.reduce(lax.psum, axes, value)]
    all_to_all x0 -> x3, blocking collectives: none -> 43 us  [summed(): row = jnp.sum(lax.all_to_all(copies, axis, 0, 0), axis=0)]
    select_n x2 -> x0, other arithmetic: 6.42 us -> none  [interaction(): jnp.take(hidden_slab.reshape(-1, feature_width), cell_index * slot_count...]
    pallas_call x0 -> x3, Pallas kernels: none -> 5.76 us  [the longest x1 2.17 us: second_layer(): pl.pallas_call(second_kernel, out_shape=(jax.ShapeDtypeStruct((1, SLOTS),...]
    unnamed x13, local copies, waits for them, and re-layouts: 0.78 us -> 4.69 us
    concatenate x8 -> x2, other arithmetic: 3.15 us -> 0.02 us  [halo(): sheet = jnp.concatenate(both_ways(row[None], 'gy'), axis=0)]
  transfers between devices with their start and end apart: 12 -> 12, of which waited for: 5 -> 5; matrix products, arithmetic and copies ran while one was open for 2% -> 2% of each run, Pallas kernels for 0% -> 1%
where the time goes in v1:
time: 133 us; the launch traced here: 132 us
  starting transfers between devices  58.8 us (44%)
  blocking collectives  43 us (32%)
  waiting for transfers between devices  15.7 us (12%)
  local copies, waits for them, and re-layouts  6.88 us (5%)
  Pallas kernels  5.76 us (4%)
    all_to_all x3, blocking collectives, summed(): row = jnp.sum(lax.all_to_all(copies, axis, 0, 0), axis=0)  43 us
    ppermute x6, starting transfers between devices, both_ways(): lax.ppermute(block, axis, backward)  41.7 us
    ppermute x6, starting transfers between devices, both_ways(): lax.ppermute(block, axis, forward)  17.1 us
    ppermute x6, waiting for transfers between devices, both_ways(): lax.ppermute(block, axis, forward)  15.7 us
    unnamed x13, local copies, waits for them, and re-layouts  4.69 us
  transfers between devices with their start and end apart: 12, of which 5 were waited for; matrix products, arithmetic and copies ran while one was open for 2% of the time, Pallas kernels for 1%

profile of v1, /device:TPU:1, one launch (start us, length us, event | category | flops | bytes accessed | tf_op | source)
XLA Modules:
  0.0 132.2 jit_solution(275974286065466925)
XLA Ops:
  0.6 0.7 bitcast_convert_fusion
  1.3 0.7 copy.17
  2.0 6.0 %collective-permute-start.1 = (f32[1,4,48]{2,1,0:T(4,128)S(1)}, f32[1,4,48]{2,1,0:T(4,128)S(1)}, u32[]{:S(2)}, u32[]{:S(2)}) collective-permute-start(f32[1,4,48]{2,1,0:T(4,128)S(1)} %maximum_bitcast_fusion.2), channel_id=1, source_target_pairs={{256,0},{512,256},{768,512},{0,768},{257,1},{513,257},{769,513},{1... | collective-permute-start | bytes 2312 | tf_op jit(solution)/shard_map/ppermute | solution.py:171
  8.0 1.9 %collective-permute-start = (f32[1,4,48]{2,1,0:T(4,128)S(1)}, f32[1,4,48]{2,1,0:T(4,128)S(1)}, u32[]{:S(2)}, u32[]{:S(2)}) collective-permute-start(f32[1,4,48]{2,1,0:T(4,128)S(1)} %maximum_bitcast_fusion.2), channel_id=1, source_target_pairs={{0,256},{256,512},{512,768},{768,0},{1,257},{257,513},{513,769},{7... | collective-permute-start | bytes 2312 | tf_op jit(solution)/shard_map/ppermute | solution.py:171
  10.0 0.0 collective-permute-done.1
  10.0 4.2 %collective-permute-done = f32[1,4,48]{2,1,0:T(4,128)S(1)} collective-permute-done((f32[1,4,48]{2,1,0:T(4,128)S(1)}, f32[1,4,48]{2,1,0:T(4,128)S(1)}, u32[]{:S(2)}, u32[]{:S(2)}) %collective-permute-start) | collective-permute-done | bytes 800 | tf_op jit(solution)/shard_map/ppermute | solution.py:171
  14.2 17.9 %collective-permute-start.3 = (f32[1,3,4,48]{3,2,1,0:T(4,128)S(1)}, f32[1,3,4,48]{3,2,1,0:T(4,128)S(1)}, u32[]{:S(2)}, u32[]{:S(2)}) collective-permute-start(f32[1,3,4,48]{3,2,1,0:T(4,128)S(1)} %maximum_bitcast_fusion.1), channel_id=1, source_target_pairs={{16,0},{32,16},{48,32},{64,48},{80,64},{96,80},{112,96},{128,112},... | collective-permute-start | bytes 6920 | tf_op jit(solution)/shard_map/ppermute | solution.py:171
  32.1 1.9 %collective-permute-start.2 = (f32[1,3,4,48]{3,2,1,0:T(4,128)S(1)}, f32[1,3,4,48]{3,2,1,0:T(4,128)S(1)}, u32[]{:S(2)}, u32[]{:S(2)}) collective-permute-start(f32[1,3,4,48]{3,2,1,0:T(4,128)S(1)} %maximum_bitcast_fusion.1), channel_id=1, source_target_pairs={{0,16},{16,32},{32,48},{48,64},{64,80},{80,96},{96,112},{112,128},... | collective-permute-start | bytes 6920 | tf_op jit(solution)/shard_map/ppermute | solution.py:171
  34.0 0.8 slice_bitcast_fusion
  34.8 0.0 collective-permute-done.3
  34.8 2.9 %collective-permute-done.2 = f32[1,3,4,48]{3,2,1,0:T(4,128)S(1)} collective-permute-done((f32[1,3,4,48]{3,2,1,0:T(4,128)S(1)}, f32[1,3,4,48]{3,2,1,0:T(4,128)S(1)}, u32[]{:S(2)}, u32[]{:S(2)}) %collective-permute-start.2) | collective-permute-done | bytes 2336 | tf_op jit(solution)/shard_map/ppermute | solution.py:171
  37.7 5.4 %collective-permute-start.5 = (f32[3,3,4,48]{3,2,1,0:T(4,128)S(1)}, f32[3,3,4,48]{3,2,1,0:T(4,128)S(1)}, u32[]{:S(2)}, u32[]{:S(2)}) collective-permute-start(f32[3,3,4,48]{3,2,1,0:T(4,128)S(1)} %pad_maximum_fusion.1), channel_id=1, source_target_pairs={{1,0},{2,1},{3,2},{4,3},{5,4},{6,5},{7,6},{8,7},{9,8},{10,9},{11,1... | collective-permute-start | bytes 20744 | tf_op jit(solution)/shard_map/ppermute | solution.py:171
  43.1 4.7 %collective-permute-start.4 = (f32[3,3,4,48]{3,2,1,0:T(4,128)S(1)}, f32[3,3,4,48]{3,2,1,0:T(4,128)S(1)}, u32[]{:S(2)}, u32[]{:S(2)}) collective-permute-start(f32[3,3,4,48]{3,2,1,0:T(4,128)S(1)} %pad_maximum_fusion.1), channel_id=1, source_target_pairs={{0,1},{1,2},{2,3},{3,4},{4,5},{5,6},{6,7},{7,8},{8,9},{9,10},{10,1... | collective-permute-start | bytes 20744 | tf_op jit(solution)/shard_map/ppermute | solution.py:171
  47.8 0.7 slice_bitcast_fusion.2
  48.5 0.7 pad.4.embedding
  49.2 0.0 copy-start
  49.2 0.7 copy-done
  49.9 0.0 copy-start.1
  49.9 0.7 copy-done.1
  50.6 1.5 %count_table.1.counts = bf16[48,1536]{1,0:T(8,128)(2,1)S(1)} custom-call(s32[48,128]{1,0:T(8,128)S(1)} %bitcast.41, s32[48]{0:T(128)S(1)} %bitcast.47), custom_call_target="tpu_custom_call" | custom-call | tf_op jit(solution)/shard_map/count_table/pallas_call | solution.py:51
  52.1 0.0 collective-permute-done.5
  52.1 0.0 collective-permute-done.4
  52.1 0.0 copy-start.2
  52.1 0.6 copy-done.2
  52.8 2.1 %first_layer.1 = (bf16[768,1536]{1,0:T(8,128)(2,1)S(1)}, bf16[48,128]{1,0:T(8,128)(2,1)S(1)}) custom-call(f32[9,4,48]{2,1,0:T(4,128)S(1)} %bitcast.43, f32[9,4,48]{2,1,0:T(4,128)S(1)} %bitcast.40, f32[9,4,48]{2,1,0:T(4,128)S(1)} %bitcast.42, bf16[48,1536]{1,0:T(8,128)(2,1)S(1)} %count_table.1.counts, f32[16]{0:T(128)S(1)} %copy-done.2, ...), custom_call_target="tpu_custom_call" | custom-call | tf_op jit(solution)/shard_map/first_layer/pallas_call | solution.py:122
  54.9 1.9 %collective-permute-start.7 = (bf16[1,48,128]{2,1,0:T(8,128)(2,1)S(1)}, bf16[1,48,128]{2,1,0:T(8,128)(2,1)S(1)}, u32[]{:S(2)}, u32[]{:S(2)}) collective-permute-start(bf16[1,48,128]{2,1,0:T(8,128)(2,1)S(1)} %bitcast.44), channel_id=1, source_target_pairs={{256,0},{512,256},{768,512},{0,768},{257,1},{513,257},{769,513},{1... | collective-permute-start | bytes 36872 | tf_op jit(solution)/shard_map/ppermute | solution.py:171
  56.8 3.4 %collective-permute-start.6 = (bf16[1,48,128]{2,1,0:T(8,128)(2,1)S(1)}, bf16[1,48,128]{2,1,0:T(8,128)(2,1)S(1)}, u32[]{:S(2)}, u32[]{:S(2)}) collective-permute-start(bf16[1,48,128]{2,1,0:T(8,128)(2,1)S(1)} %bitcast.45), channel_id=1, source_target_pairs={{0,256},{256,512},{512,768},{768,0},{1,257},{257,513},{513,769},{7... | collective-permute-start | bytes 36872 | tf_op jit(solution)/shard_map/ppermute | solution.py:171
  60.2 0.0 collective-permute-done.7
  60.2 2.9 %collective-permute-done.6 = bf16[1,48,128]{2,1,0:T(8,128)(2,1)S(1)} collective-permute-done((bf16[1,48,128]{2,1,0:T(8,128)(2,1)S(1)}, bf16[1,48,128]{2,1,0:T(8,128)(2,1)S(1)}, u32[]{:S(2)}, u32[]{:S(2)}) %collective-permute-start.6) | collective-permute-done | bytes 12320 | tf_op jit(solution)/shard_map/ppermute | solution.py:171
  63.0 1.9 %collective-permute-start.9 = (bf16[1,3,48,128]{3,2,1,0:T(8,128)(2,1)S(1)}, bf16[1,3,48,128]{3,2,1,0:T(8,128)(2,1)S(1)}, u32[]{:S(2)}, u32[]{:S(2)}) collective-permute-start(bf16[1,3,48,128]{3,2,1,0:T(8,128)(2,1)S(1)} %maximum_bitcast_fusion), channel_id=1, source_target_pairs={{16,0},{32,16},{48,32},{64,48},{80,64},{96,80},{112,96},{128,112},... | collective-permute-start | bytes 110600 | tf_op jit(solution)/shard_map/ppermute | solution.py:171
  65.0 3.4 %collective-permute-start.8 = (bf16[1,3,48,128]{3,2,1,0:T(8,128)(2,1)S(1)}, bf16[1,3,48,128]{3,2,1,0:T(8,128)(2,1)S(1)}, u32[]{:S(2)}, u32[]{:S(2)}) collective-permute-start(bf16[1,3,48,128]{3,2,1,0:T(8,128)(2,1)S(1)} %maximum_bitcast_fusion), channel_id=1, source_target_pairs={{0,16},{16,32},{32,48},{48,64},{64,80},{80,96},{96,112},{112,128},... | collective-permute-start | bytes 110600 | tf_op jit(solution)/shard_map/ppermute | solution.py:171
  68.3 0.0 collective-permute-done.9
  68.3 2.5 %collective-permute-done.8 = bf16[1,3,48,128]{3,2,1,0:T(8,128)(2,1)S(1)} collective-permute-done((bf16[1,3,48,128]{3,2,1,0:T(8,128)(2,1)S(1)}, bf16[1,3,48,128]{3,2,1,0:T(8,128)(2,1)S(1)}, u32[]{:S(2)}, u32[]{:S(2)}) %collective-permute-start.8) | collective-permute-done | bytes 36896 | tf_op jit(solution)/shard_map/ppermute | solution.py:171
  70.9 8.5 %collective-permute-start.11 = (bf16[3,3,48,128]{3,2,1,0:T(8,128)(2,1)S(1)}, bf16[3,3,48,128]{3,2,1,0:T(8,128)(2,1)S(1)}, u32[]{:S(2)}, u32[]{:S(2)}) collective-permute-start(bf16[3,3,48,128]{3,2,1,0:T(8,128)(2,1)S(1)} %pad_maximum_fusion), channel_id=1, source_target_pairs={{1,0},{2,1},{3,2},{4,3},{5,4},{6,5},{7,6},{8,7},{9,8},{10,9},{11,1... | collective-permute-start | bytes 331784 | tf_op jit(solution)/shard_map/ppermute | solution.py:171
  79.4 1.9 %collective-permute-start.10 = (bf16[3,3,48,128]{3,2,1,0:T(8,128)(2,1)S(1)}, bf16[3,3,48,128]{3,2,1,0:T(8,128)(2,1)S(1)}, u32[]{:S(2)}, u32[]{:S(2)}) collective-permute-start(bf16[3,3,48,128]{3,2,1,0:T(8,128)(2,1)S(1)} %pad_maximum_fusion), channel_id=1, source_target_pairs={{0,1},{1,2},{2,3},{3,4},{4,5},{5,6},{6,7},{7,8},{8,9},{9,10},{10,1... | collective-permute-start | bytes 331784 | tf_op jit(solution)/shard_map/ppermute | solution.py:171
  81.3 0.0 collective-permute-done.11
  81.3 3.2 %collective-permute-done.10 = bf16[3,3,48,128]{3,2,1,0:T(8,128)(2,1)S(1)} collective-permute-done((bf16[3,3,48,128]{3,2,1,0:T(8,128)(2,1)S(1)}, bf16[3,3,48,128]{3,2,1,0:T(8,128)(2,1)S(1)}, u32[]{:S(2)}, u32[]{:S(2)}) %collective-permute-start.10) | collective-permute-done | bytes 110624 | tf_op jit(solution)/shard_map/ppermute | solution.py:171
  84.5 0.0 copy-start.3
  84.5 0.7 copy-done.3
  85.2 0.0 copy-start.4
  85.2 0.7 copy-done.4
  85.8 0.0 copy-start.5
  85.8 0.7 copy-done.5
  86.5 2.2 %second_layer.1 = (f32[1,48]{1,0:T(1,128)}, f32[1,128]{1,0:T(1,128)S(1)}) custom-call(bf16[768,1536]{1,0:T(8,128)(2,1)S(1)} %get-tuple-element.6.edges, bf16[432,128]{1,0:T(8,128)(2,1)S(1)} %bitcast.39, bf16[432,128]{1,0:T(8,128)(2,1)S(1)} %bitcast.37, bf16[432,128]{1,0:T(8,128)(2,1)S(1)} %bitcast.38, bf16[16,128]{1,0:T(8,128)(2,1)S(1)} %get-tuple-element.12.radial, ...), custom_call_target="tpu_custom_call" | custom-call | tf_op jit(solution)/shard_map/second_layer/pallas_call | solution.py:154
  88.6 6.8 %all_to_all.15 = f32[4,1,128]{2,1,0:T(1,128)S(1)} all-to-all(f32[4,1,128]{2,1,0:T(1,128)S(1)} %broadcast_in_dim.37), channel_id=1, replica_groups=mesh['gx'=4,'gy'=16,'gz'=16] {'gx'}, dimensions={0} | all-to-all | bytes 4096 | tf_op jit(solution)/shard_map/all_to_all | solution.py:183
  95.4 14.0 %all_to_all.16 = f32[16,1,128]{2,1,0:T(1,128)S(1)} all-to-all(f32[16,1,128]{2,1,0:T(1,128)S(1)} %broadcast_in_dim.38), channel_id=1, replica_groups=mesh['gx'=4,'gy'=16,'gz'=16] {'gy'}, dimensions={0} | all-to-all | bytes 16384 | tf_op jit(solution)/shard_map/all_to_all | solution.py:183
  109.4 22.3 %all_to_all.17 = f32[16,1,128]{2,1,0:T(1,128)S(1)} all-to-all(f32[16,1,128]{2,1,0:T(1,128)S(1)} %broadcast_in_dim.39), channel_id=1, replica_groups=mesh['gx'=4,'gy'=16,'gz'=16] {'gz'}, dimensions={0} | all-to-all | bytes 16384 | tf_op jit(solution)/shard_map/all_to_all | solution.py:183
  131.7 0.5 reduce_sum.31
  (10 shorter events, 0.1 us)
Async XLA Ops:
  2.0 8.0 %collective-permute-start.1 = (f32[1,4,48]{2,1,0:T(4,128)S(1)}, f32[1,4,48]{2,1,0:T(4,128)S(1)}, u32[]{:S(2)}, u32[]{:S(2)}) collective-permute-start(f32[1,4,48]{2,1,0:T(4,128)S(1)} %maximum_bitcast_fusion.2), channel_id=1, source_target_pairs={{256,0},{512,256},{768,512},{0,768},{257,1},{513,257},{769,513},{1... | collective-permute-start | bytes 2312 | tf_op jit(solution)/shard_map/ppermute | solution.py:171
  8.0 6.1 %collective-permute-start = (f32[1,4,48]{2,1,0:T(4,128)S(1)}, f32[1,4,48]{2,1,0:T(4,128)S(1)}, u32[]{:S(2)}, u32[]{:S(2)}) collective-permute-start(f32[1,4,48]{2,1,0:T(4,128)S(1)} %maximum_bitcast_fusion.2), channel_id=1, source_target_pairs={{0,256},{256,512},{512,768},{768,0},{1,257},{257,513},{513,769},{7... | collective-permute-start | bytes 2312 | tf_op jit(solution)/shard_map/ppermute | solution.py:171
  14.2 20.7 %collective-permute-start.3 = (f32[1,3,4,48]{3,2,1,0:T(4,128)S(1)}, f32[1,3,4,48]{3,2,1,0:T(4,128)S(1)}, u32[]{:S(2)}, u32[]{:S(2)}) collective-permute-start(f32[1,3,4,48]{3,2,1,0:T(4,128)S(1)} %maximum_bitcast_fusion.1), channel_id=1, source_target_pairs={{16,0},{32,16},{48,32},{64,48},{80,64},{96,80},{112,96},{128,112},... | collective-permute-start | bytes 6920 | tf_op jit(solution)/shard_map/ppermute | solution.py:171
  32.1 5.6 %collective-permute-start.2 = (f32[1,3,4,48]{3,2,1,0:T(4,128)S(1)}, f32[1,3,4,48]{3,2,1,0:T(4,128)S(1)}, u32[]{:S(2)}, u32[]{:S(2)}) collective-permute-start(f32[1,3,4,48]{3,2,1,0:T(4,128)S(1)} %maximum_bitcast_fusion.1), channel_id=1, source_target_pairs={{0,16},{16,32},{32,48},{48,64},{64,80},{80,96},{96,112},{112,128},... | collective-permute-start | bytes 6920 | tf_op jit(solution)/shard_map/ppermute | solution.py:171
  37.7 14.4 %collective-permute-start.5 = (f32[3,3,4,48]{3,2,1,0:T(4,128)S(1)}, f32[3,3,4,48]{3,2,1,0:T(4,128)S(1)}, u32[]{:S(2)}, u32[]{:S(2)}) collective-permute-start(f32[3,3,4,48]{3,2,1,0:T(4,128)S(1)} %pad_maximum_fusion.1), channel_id=1, source_target_pairs={{1,0},{2,1},{3,2},{4,3},{5,4},{6,5},{7,6},{8,7},{9,8},{10,9},{11,1... | collective-permute-start | bytes 20744 | tf_op jit(solution)/shard_map/ppermute | solution.py:171
  43.1 9.0 %collective-permute-start.4 = (f32[3,3,4,48]{3,2,1,0:T(4,128)S(1)}, f32[3,3,4,48]{3,2,1,0:T(4,128)S(1)}, u32[]{:S(2)}, u32[]{:S(2)}) collective-permute-start(f32[3,3,4,48]{3,2,1,0:T(4,128)S(1)} %pad_maximum_fusion.1), channel_id=1, source_target_pairs={{0,1},{1,2},{2,3},{3,4},{4,5},{5,6},{6,7},{7,8},{8,9},{9,10},{10,1... | collective-permute-start | bytes 20744 | tf_op jit(solution)/shard_map/ppermute | solution.py:171
  49.2 0.7 copy-start
  49.9 0.7 copy-start.1
  52.1 0.7 copy-start.2
  54.9 5.3 %collective-permute-start.7 = (bf16[1,48,128]{2,1,0:T(8,128)(2,1)S(1)}, bf16[1,48,128]{2,1,0:T(8,128)(2,1)S(1)}, u32[]{:S(2)}, u32[]{:S(2)}) collective-permute-start(bf16[1,48,128]{2,1,0:T(8,128)(2,1)S(1)} %bitcast.44), channel_id=1, source_target_pairs={{256,0},{512,256},{768,512},{0,768},{257,1},{513,257},{769,513},{1... | collective-permute-start | bytes 36872 | tf_op jit(solution)/shard_map/ppermute | solution.py:171
  56.8 6.2 %collective-permute-start.6 = (bf16[1,48,128]{2,1,0:T(8,128)(2,1)S(1)}, bf16[1,48,128]{2,1,0:T(8,128)(2,1)S(1)}, u32[]{:S(2)}, u32[]{:S(2)}) collective-permute-start(bf16[1,48,128]{2,1,0:T(8,128)(2,1)S(1)} %bitcast.45), channel_id=1, source_target_pairs={{0,256},{256,512},{512,768},{768,0},{1,257},{257,513},{513,769},{7... | collective-permute-start | bytes 36872 | tf_op jit(solution)/shard_map/ppermute | solution.py:171
  63.0 5.3 %collective-permute-start.9 = (bf16[1,3,48,128]{3,2,1,0:T(8,128)(2,1)S(1)}, bf16[1,3,48,128]{3,2,1,0:T(8,128)(2,1)S(1)}, u32[]{:S(2)}, u32[]{:S(2)}) collective-permute-start(bf16[1,3,48,128]{3,2,1,0:T(8,128)(2,1)S(1)} %maximum_bitcast_fusion), channel_id=1, source_target_pairs={{16,0},{32,16},{48,32},{64,48},{80,64},{96,80},{112,96},{128,112},... | collective-permute-start | bytes 110600 | tf_op jit(solution)/shard_map/ppermute | solution.py:171
  65.0 5.9 %collective-permute-start.8 = (bf16[1,3,48,128]{3,2,1,0:T(8,128)(2,1)S(1)}, bf16[1,3,48,128]{3,2,1,0:T(8,128)(2,1)S(1)}, u32[]{:S(2)}, u32[]{:S(2)}) collective-permute-start(bf16[1,3,48,128]{3,2,1,0:T(8,128)(2,1)S(1)} %maximum_bitcast_fusion), channel_id=1, source_target_pairs={{0,16},{16,32},{32,48},{48,64},{64,80},{80,96},{96,112},{112,128},... | collective-permute-start | bytes 110600 | tf_op jit(solution)/shard_map/ppermute | solution.py:171
  70.9 10.4 %collective-permute-start.11 = (bf16[3,3,48,128]{3,2,1,0:T(8,128)(2,1)S(1)}, bf16[3,3,48,128]{3,2,1,0:T(8,128)(2,1)S(1)}, u32[]{:S(2)}, u32[]{:S(2)}) collective-permute-start(bf16[3,3,48,128]{3,2,1,0:T(8,128)(2,1)S(1)} %pad_maximum_fusion), channel_id=1, source_target_pairs={{1,0},{2,1},{3,2},{4,3},{5,4},{6,5},{7,6},{8,7},{9,8},{10,9},{11,1... | collective-permute-start | bytes 331784 | tf_op jit(solution)/shard_map/ppermute | solution.py:171
  79.4 5.1 %collective-permute-start.10 = (bf16[3,3,48,128]{3,2,1,0:T(8,128)(2,1)S(1)}, bf16[3,3,48,128]{3,2,1,0:T(8,128)(2,1)S(1)}, u32[]{:S(2)}, u32[]{:S(2)}) collective-permute-start(bf16[3,3,48,128]{3,2,1,0:T(8,128)(2,1)S(1)} %pad_maximum_fusion), channel_id=1, source_target_pairs={{0,1},{1,2},{2,3},{3,4},{4,5},{5,6},{6,7},{7,8},{8,9},{9,10},{10,1... | collective-permute-start | bytes 331784 | tf_op jit(solution)/shard_map/ppermute | solution.py:171
  84.5 0.7 copy-start.3
  85.2 0.7 copy-start.4
  85.8 0.7 copy-start.5

commit v2 on v1

v2 whole, which is shorter than its diff:
```python
import jax
import jax.numpy as jnp
from jax import lax
from jax.experimental import pallas as pl
from jax.experimental.pallas import tpu as pltpu
from jax.sharding import PartitionSpec as P

F = 128
NB = 128
NRBF = 16
SLOTS = 48
LAYERS = 2
PLANE = 9 * SLOTS
LANES = 512
TILES = 3 * LANES // 128
NX, NY, NZ = 4, 16, 16
SHEET = NX * NZ
AXES = ("gx", "gy", "gz")
SMALL = pltpu.CompilerParams(vmem_limit_bytes=16 * 1024 * 1024)
VMEM = pl.BlockSpec(memory_space=pltpu.VMEM)
HBM = pl.BlockSpec(memory_space=pltpu.HBM)


def side(axis):
    return 1 - 2 * (lax.axis_index(axis) & 1)


def kept(array):
    return pltpu.with_memory_space_constraint(array, pltpu.VMEM)


def outside(array):
    return pltpu.with_memory_space_constraint(array, pltpu.HBM)


def fetch(sources, targets, semaphores):
    copies = [
        pltpu.make_async_copy(source, target, semaphores.at[i])
        for i, (source, target) in enumerate(zip(sources, targets))
    ]
    for copy in copies:
        copy.start()
    for copy in copies:
        copy.wait()


def pack_kernel(positions, species, out, places, kinds, semaphores):
    fetch((positions, species), (places, kinds), semaphores)
    rows = [places[d] for d in range(3)] + [kinds[...].astype(jnp.float32)]
    record = jnp.concatenate(rows, axis=1)
    for i in range(SHEET):
        out[i] = record


def packed(positions, species):
    return pl.pallas_call(
        pack_kernel,
        out_shape=pltpu.VMEM((SHEET, 1, 4 * SLOTS), jnp.float32),
        in_specs=[HBM, HBM],
        out_specs=VMEM,
        scratch_shapes=[
            pltpu.VMEM((3, 1, SLOTS), jnp.float32),
            pltpu.VMEM((1, SLOTS), jnp.int32),
            pltpu.SemaphoreType.DMA((2,)),
        ],
        compiler_params=SMALL,
        name="pack_records",
    )(outside(positions), outside(species))


def pick_kernel(records, out):
    x = lax.axis_index("gx")
    z = lax.axis_index("gz")
    for i in range(3):
        row = (x + (i - 1) * side("gx")) & (NX - 1)
        for k in range(3):
            record = records[row * NZ + ((z + (k - 1) * side("gz")) & (NZ - 1))]
            for d in range(4):
                out[i * 3 + k, d : d + 1] = record[:, d * SLOTS : (d + 1) * SLOTS]


def picked(records):
    return pl.pallas_call(
        pick_kernel,
        out_shape=pltpu.VMEM((9, 4, SLOTS), jnp.float32),
        in_specs=[VMEM],
        out_specs=VMEM,
        compiler_params=SMALL,
        name="pick_records",
    )(kept(records))


def prepare_kernel(
    neighbours,
    neigh_counts,
    species,
    embedding,
    decay,
    radial,
    weight,
    readout,
    bias,
    out,
    rates,
    filters,
    updates,
    kinds,
    ends,
    codes,
    counts,
    kind,
    rows,
    scales,
    narrow,
    last,
    offsets,
    high,
    low,
    table,
    semaphores,
):
    fetch(
        (neighbours, neigh_counts, species, embedding, decay, radial, weight, readout, bias),
        (codes, counts, kind, rows, scales, narrow, updates, last, offsets),
        semaphores,
    )
    code = codes[...]
    offset = (code * 1366) >> 16
    slot = code - offset * SLOTS
    across = (offset * 171) >> 9
    depth = (across * 171) >> 9
    x = 1 + (depth - 1) * side("gx")
    y = 1 + (across - depth * 3 - 1) * side("gy")
    z = 1 + (offset - across * 3 - 1) * side("gz")
    place = y * LANES + (x * 3 + z) * SLOTS + slot
    high[...] = place >> 7
    low[...] = place & 127
    lane = lax.broadcasted_iota(jnp.int32, (1, NB), 1)
    tile_of = lax.broadcasted_iota(jnp.int32, (16, NB), 0)
    lane_of = lax.broadcasted_iota(jnp.int32, (128, NB), 0)
    for atom in range(SLOTS):
        tile = jnp.where(lane < counts[atom], high[atom : atom + 1], -1)
        left = jnp.where(tile == tile_of, 1.0, 0.0).astype(jnp.bfloat16)
        right = jnp.where(low[atom : atom + 1] == lane_of, 1.0, 0.0).astype(jnp.bfloat16)
        table[atom * 16 : atom * 16 + 16] = lax.dot_general(
            left, right, (((1,), (1,)), ((), ())), preferred_element_type=jnp.float32
        )
    for tile in range(TILES):
        out[:, tile * 128 : tile * 128 + 128] = table[pl.ds(tile, SLOTS, stride=16), :].astype(
            jnp.bfloat16
        )
    for b in range(NRBF):
        rates[b : b + 1] = jnp.full((1, LANES), -scales[b], jnp.float32)
    filters[...] = narrow[...].astype(jnp.float32)
    known = rows[...].astype(jnp.float32)
    kinds[...] = jnp.concatenate([known, jnp.zeros((4, F), jnp.float32)], axis=0).astype(
        jnp.bfloat16
    )
    ends[0:1] = last[...].astype(jnp.float32)
    shift = jnp.zeros((1, SLOTS), jnp.float32)
    for k in range(4):
        shift = shift + jnp.where(kind[...] == k, offsets[k], 0.0)
    ends[1:2, 0:SLOTS] = shift


def prepared(*arrays):
    return pl.pallas_call(
        prepare_kernel,
        out_shape=(
            pltpu.VMEM((SLOTS, 3 * LANES), jnp.bfloat16),
            pltpu.VMEM((NRBF, LANES), jnp.float32),
            pltpu.VMEM((LAYERS, NRBF, F), jnp.float32),
            pltpu.VMEM((LAYERS, F, F), jnp.bfloat16),
            pltpu.VMEM((8, F), jnp.bfloat16),
            pltpu.VMEM((2, F), jnp.float32),
        ),
        in_specs=[HBM] * 9,
        out_specs=(VMEM,) * 6,
        scratch_shapes=[
            pltpu.VMEM((SLOTS, NB), jnp.int32),
            pltpu.SMEM((SLOTS,), jnp.int32),
            pltpu.VMEM((1, SLOTS), jnp.int32),
            pltpu.VMEM((4, F), jnp.bfloat16),
            pltpu.SMEM((NRBF,), jnp.float32),
            pltpu.VMEM((LAYERS, NRBF, F), jnp.bfloat16),
            pltpu.VMEM((1, F), jnp.bfloat16),
            pltpu.SMEM((4,), jnp.float32),
            pltpu.VMEM((SLOTS, NB), jnp.int32),
            pltpu.VMEM((SLOTS, NB), jnp.int32),
            pltpu.VMEM((SLOTS * 16, 128), jnp.float32),
            pltpu.SemaphoreType.DMA((9,)),
        ],
        compiler_params=SMALL,
        name="prepare",
    )(*map(outside, arrays))


def node_update(edges, tables, weights, weight):
    message = jnp.zeros((SLOTS, F), jnp.float32)
    gathered = None
    for y in range(3):
        part = jnp.dot(
            edges[:, y * LANES : y * LANES + PLANE],
            tables[y],
            preferred_element_type=jnp.float32,
        )
        gathered = part if gathered is None else gathered + part
    for b in range(NRBF):
        message = message + gathered[b * SLOTS : (b + 1) * SLOTS] * weights[b : b + 1]
    scale = lax.rsqrt(jnp.mean(message * message, axis=1, keepdims=True) + 1e-05)
    normed = (message * scale).astype(jnp.bfloat16)
    moved = jnp.dot(normed, weight, preferred_element_type=jnp.float32)
    own = tables[1][4 * SLOTS : 5 * SLOTS].astype(jnp.float32)
    return (own + moved / (1.0 + jnp.exp(-moved))).astype(jnp.bfloat16)


def first_kernel(
    before, middle, after, counts, rates, embedding, radial, weight, edges, hidden
):
    kinds = embedding[...]
    kind_of = lax.broadcasted_iota(jnp.int32, (8, LANES), 0).astype(jnp.float32)
    cell = lax.broadcasted_iota(jnp.int32, (4, LANES), 1) // SLOTS
    part_of = lax.broadcasted_iota(jnp.int32, (4, LANES), 0)
    across = (cell // 3 - 1) * side("gx")
    along = (cell % 3 - 1) * side("gz")
    centre = jnp.transpose(middle[4])
    tables = []
    for y, records in enumerate((before, middle, after)):
        pieces = [records[c] for c in range(9)]
        pieces.append(jnp.zeros((4, LANES - PLANE), jnp.float32))
        rows = jnp.concatenate(pieces, axis=1)
        shift = jnp.where(
            part_of == 0, across, jnp.where(part_of == 1, (y - 1) * side("gy"), along)
        )
        moved = rows + shift.astype(jnp.float32)
        squared = None
        for d in range(3):
            away = moved[d : d + 1] - centre[:, d : d + 1]
            squared = away * away if squared is None else squared + away * away
        times = counts[:, y * LANES : (y + 1) * LANES]
        for b in range(NRBF):
            basis = jnp.exp(squared * rates[b : b + 1]).astype(jnp.bfloat16)
            edges[b * SLOTS : (b + 1) * SLOTS, y * LANES : (y + 1) * LANES] = basis * times
        one_hot = jnp.where(rows[3:4] == kind_of, 1.0, 0.0)
        one_hot = jnp.transpose(one_hot).astype(jnp.bfloat16)
        table = jnp.dot(one_hot, kinds, preferred_element_type=jnp.float32)
        tables.append(table[:PLANE].astype(jnp.bfloat16))
    hidden[0] = node_update(edges, tables, radial[0], weight[0])


def first_layer(records, counts, rates, embedding, radial, weight):
    return pl.pallas_call(
        first_kernel,
        out_shape=(
            pltpu.VMEM((NRBF * SLOTS, 3 * LANES), jnp.bfloat16),
            pltpu.VMEM((1, SLOTS, F), jnp.bfloat16),
        ),
        in_specs=[VMEM] * 8,
        out_specs=(VMEM, VMEM),
        compiler_params=SMALL,
        name="first_layer",
    )(*map(kept, (*records, counts, rates, embedding, radial, weight)))


def second_kernel(edges, before, middle, after, radial, weight, ends, energy, total):
    tables = [before[...], middle[...], after[...]]
    hidden = node_update(edges, tables, radial[1], weight[1])
    terms = hidden.astype(jnp.float32) * ends[0:1]
    per_atom = jnp.sum(jnp.transpose(terms), axis=0, keepdims=True)
    result = per_atom + ends[1:2, 0:SLOTS]
    energy[...] = result
    total[...] = jnp.broadcast_to(jnp.sum(result, axis=1, keepdims=True), (1, 128))


def second_layer(edges, tables, radial, weight, ends):
    return pl.pallas_call(
        second_kernel,
        out_shape=(
            jax.ShapeDtypeStruct((1, SLOTS), jnp.float32),
            pltpu.VMEM((1, 128), jnp.float32),
        ),
        in_specs=[VMEM] * 7,
        out_specs=(VMEM, VMEM),
        compiler_params=SMALL,
        name="second_layer",
    )(*map(kept, (edges, *tables, radial, weight, ends)))


def both_sides(block, axis):
    count = lax.axis_size(axis)
    near = [(i, i ^ 1) for i in range(count)]
    far = [(i, (i - 1 + 2 * (i & 1)) % count) for i in range(count)]
    return lax.ppermute(block, axis, far), block, lax.ppermute(block, axis, near)


def halo(block):
    line = jnp.concatenate(both_sides(block, "gz"), axis=0)
    sheet = jnp.concatenate(both_sides(line[None], "gx"), axis=0)
    return both_sides(sheet, "gy")


def summed(row):
    for axes in (("gx", "gz"), ("gy",)):
        copies = jnp.broadcast_to(row[None], (lax.axis_size(axes),) + row.shape)
        row = jnp.sum(lax.all_to_all(copies, axes, 0, 0), axis=0)
    return row


def body(
    positions,
    species,
    neighbours,
    neigh_counts,
    embedding,
    rbf_decay,
    radial_weight,
    node_weight,
    readout,
    species_bias,
):
    kinds = species.reshape(1, SLOTS)
    records = packed(positions.reshape(3, 1, SLOTS), kinds)
    records = picked(lax.all_to_all(records, ("gx", "gz"), 0, 0))
    places = both_sides(records, "gy")
    counts, rates, filters, updates, embedded, ends = prepared(
        neighbours.reshape(SLOTS, NB),
        neigh_counts.reshape(SLOTS),
        kinds,
        embedding,
        rbf_decay,
        radial_weight,
        node_weight,
        readout.reshape(1, F),
        species_bias,
    )
    edges, hidden = first_layer(places, counts, rates, embedded, filters, updates)
    tables = [part.reshape(PLANE, F) for part in halo(hidden)]
    energy, total = second_layer(edges, tables, filters, updates, ends)
    return energy.reshape(1, 1, 1, SLOTS), summed(total)[0, 0]


def solution(mesh):
    split = P("gx", "gy", "gz")
    in_specs = (split, split, split, split, P(), P(), P(), P(), P(), P())
    return jax.shard_map(
        body, mesh=mesh, in_specs=in_specs, out_specs=(split, P()), check_vma=False
    )
```

time: 133 us -> 113 us (0.85)
  starting transfers between devices: 58.8 us -> 31.4 us
  blocking collectives: 43 us -> 61.8 us
  local copies, waits for them, and re-layouts: 6.88 us -> 0.03 us
  waiting for transfers between devices: 15.7 us -> 12 us
    ppermute x12 -> x8, starting transfers between devices: 58.8 us -> 31.4 us  [the longest x4 22.3 us: both_sides(): lax.ppermute(block, axis, far)]
    all_to_all x3, blocking collectives: 43 us -> 61.8 us  [the longest x2 34.5 us: summed(): row = jnp.sum(lax.all_to_all(copies, axes, 0, 0), axis=0)]
    unnamed x13 -> x0, local copies, waits for them, and re-layouts: 4.69 us -> none
    ppermute x12 -> x8, waiting for transfers between devices: 15.7 us -> 12 us  [the longest x4 12 us: both_sides(): lax.ppermute(block, axis, far)]
    squeeze x2 -> x0, local copies, waits for them, and re-layouts: 1.49 us -> none  [the longest x1 0.78 us: body(): node_weight[1]]
    pallas_call x1 -> x3, Pallas kernels: 1.51 us -> 2.88 us  [the longest x1 1.99 us: prepared(): pl.pallas_call(prepare_kernel, out_shape=(pltpu.VMEM((SLOTS, 3 * LANES),...]
  transfers between devices with their start and end apart: 12 -> 8, of which waited for: 5 -> 3; matrix products, arithmetic and copies ran while one was open for 2% -> 0% of each run, Pallas kernels for 1% -> 2%
where the time goes in v2:
time: 113 us
  blocking collectives  61.8 us (55%)
  starting transfers between devices  31.4 us (28%)
  waiting for transfers between devices  12 us (11%)
  Pallas kernels  6.06 us (5%)
    all_to_all x2, blocking collectives, summed(): row = jnp.sum(lax.all_to_all(copies, axes, 0, 0), axis=0)  34.5 us
    all_to_all x1, blocking collectives, body(): records = picked(lax.all_to_all(records, ('gx', 'gz'), 0, 0))  27.3 us
    ppermute x4, starting transfers between devices, both_sides(): lax.ppermute(block, axis, far)  22.3 us
    ppermute x4, waiting for transfers between devices, both_sides(): lax.ppermute(block, axis, far)  12 us
    ppermute x4, starting transfers between devices, both_sides(): lax.ppermute(block, axis, near)  9.11 us
  transfers between devices with their start and end apart: 8, of which 3 were waited for; matrix products, arithmetic and copies ran while one was open for 0% of the time, Pallas kernels for 2%

profile of v2, /device:TPU:1, one launch (start us, length us, event | category | flops | bytes accessed | tf_op | source)
XLA Modules:
  0.0 112.6 jit_solution(12093594512383761090)
XLA Ops:
  0.6 0.8 pack_records.1
  1.4 27.3 %all_to_all.15.records = f32[64,1,192]{2,1,0:T(1,128)S(1)} all-to-all(f32[64,1,192]{2,1,0:T(1,128)S(1)} %pack_records.1), channel_id=1, replica_groups=mesh['gx'=4,'gy'=16,'gz'=16] {'gx','gz'}, dimensions={0} | all-to-all | bytes 98304 | tf_op jit(solution)/shard_map/all_to_all | solution.py:323
  28.7 0.1 pick_records.1.middle
  28.8 1.9 %collective-permute-start.1 = (f32[9,4,48]{2,1,0:T(4,128)S(1)}, f32[9,4,48]{2,1,0:T(4,128)S(1)}, u32[]{:S(2)}, u32[]{:S(2)}) collective-permute-start(f32[9,4,48]{2,1,0:T(4,128)S(1)} %pick_records.1.middle), channel_id=1, source_target_pairs={{0,16},{16,0},{32,48},{48,32},{64,80},{80,64},{96,112},{112,96},{1... | collective-permute-start | bytes 20744 | tf_op jit(solution)/shard_map/ppermute | solution.py:293
  30.7 12.2 %collective-permute-start = (f32[9,4,48]{2,1,0:T(4,128)S(1)}, f32[9,4,48]{2,1,0:T(4,128)S(1)}, u32[]{:S(2)}, u32[]{:S(2)}) collective-permute-start(f32[9,4,48]{2,1,0:T(4,128)S(1)} %pick_records.1.middle), channel_id=1, source_target_pairs={{0,240},{16,32},{32,16},{48,64},{64,48},{80,96},{96,80},{112,128},... | collective-permute-start | bytes 20744 | tf_op jit(solution)/shard_map/ppermute | solution.py:293
  42.9 2.0 %prepare.1 = (bf16[48,1536]{1,0:T(8,128)(2,1)S(1)}, f32[16,512]{1,0:T(8,128)S(1)}, f32[2,16,128]{2,1,0:T(8,128)S(1)}, bf16[2,128,128]{2,1,0:T(8,128)(2,1)S(1)}, ...) custom-call(s32[48,128]{1,0:T(8,128)} %bitcast.23, s32[48]{0:T(128)} %bitcast.27, s32[1,48]{1,0:T(1,128)} %bitcast.25, ...), custom_call_target="tpu_custom_call" | custom-call | tf_op jit(solution)/shard_map/prepare/pallas_call | solution.py:167
  44.9 0.0 collective-permute-done.1.after
  44.9 0.0 collective-permute-done.before
  45.0 1.5 %first_layer.1 = (bf16[768,1536]{1,0:T(8,128)(2,1)S(1)}, bf16[1,48,128]{2,1,0:T(8,128)(2,1)S(1)}) custom-call(f32[9,4,48]{2,1,0:T(4,128)S(1)} %collective-permute-done.before, f32[9,4,48]{2,1,0:T(4,128)S(1)} %pick_records.1.middle, f32[9,4,48]{2,1,0:T(4,128)S(1)} %collective-permute-done.1.after, bf16[48,1536]{1,0:T(8,128)(2,1)S(1)} %get-tuple-element.12.counts, ...), custom_call_target="tpu_custom_call" | custom-call | tf_op jit(solution)/shard_map/first_layer/pallas_call | solution.py:252
  46.5 2.9 %collective-permute-start.3 = (bf16[1,48,128]{2,1,0:T(8,128)(2,1)S(1)}, bf16[1,48,128]{2,1,0:T(8,128)(2,1)S(1)}, u32[]{:S(2)}, u32[]{:S(2)}) collective-permute-start(bf16[1,48,128]{2,1,0:T(8,128)(2,1)S(1)} %get-tuple-element.18), channel_id=1, source_target_pairs={{0,1},{1,0},{2,3},{3,2},{4,5},{5,4},{6,7},{7,6},{8,9},{9,8},{10,11... | collective-permute-start | bytes 36872 | tf_op jit(solution)/shard_map/ppermute | solution.py:293
  49.4 2.3 %collective-permute-start.2 = (bf16[1,48,128]{2,1,0:T(8,128)(2,1)S(1)}, bf16[1,48,128]{2,1,0:T(8,128)(2,1)S(1)}, u32[]{:S(2)}, u32[]{:S(2)}) collective-permute-start(bf16[1,48,128]{2,1,0:T(8,128)(2,1)S(1)} %get-tuple-element.18), channel_id=1, source_target_pairs={{0,15},{1,2},{2,1},{3,4},{4,3},{5,6},{6,5},{7,8},{8,7},{9,10},{10,... | collective-permute-start | bytes 36872 | tf_op jit(solution)/shard_map/ppermute | solution.py:293
  51.7 0.0 collective-permute-done.3
  51.7 6.6 %collective-permute-done.2 = bf16[1,48,128]{2,1,0:T(8,128)(2,1)S(1)} collective-permute-done((bf16[1,48,128]{2,1,0:T(8,128)(2,1)S(1)}, bf16[1,48,128]{2,1,0:T(8,128)(2,1)S(1)}, u32[]{:S(2)}, u32[]{:S(2)}) %collective-permute-start.2) | collective-permute-done | bytes 12320 | tf_op jit(solution)/shard_map/ppermute | solution.py:293
  58.3 2.4 %collective-permute-start.5 = (bf16[1,3,48,128]{3,2,1,0:T(8,128)(2,1)S(1)}, bf16[1,3,48,128]{3,2,1,0:T(8,128)(2,1)S(1)}, u32[]{:S(2)}, u32[]{:S(2)}) collective-permute-start(bf16[1,3,48,128]{3,2,1,0:T(8,128)(2,1)S(1)} %maximum_bitcast_fusion), channel_id=1, source_target_pairs={{0,256},{256,0},{512,768},{768,512},{1,257},{257,1},{513,769},{769... | collective-permute-start | bytes 110600 | tf_op jit(solution)/shard_map/ppermute | solution.py:293
  60.7 3.2 %collective-permute-start.4 = (bf16[1,3,48,128]{3,2,1,0:T(8,128)(2,1)S(1)}, bf16[1,3,48,128]{3,2,1,0:T(8,128)(2,1)S(1)}, u32[]{:S(2)}, u32[]{:S(2)}) collective-permute-start(bf16[1,3,48,128]{3,2,1,0:T(8,128)(2,1)S(1)} %maximum_bitcast_fusion), channel_id=1, source_target_pairs={{0,768},{256,512},{512,256},{768,0},{1,769},{257,513},{513,257},{7... | collective-permute-start | bytes 110600 | tf_op jit(solution)/shard_map/ppermute | solution.py:293
  63.9 0.0 collective-permute-done.5
  63.9 3.3 %collective-permute-done.4 = bf16[1,3,48,128]{3,2,1,0:T(8,128)(2,1)S(1)} collective-permute-done((bf16[1,3,48,128]{3,2,1,0:T(8,128)(2,1)S(1)}, bf16[1,3,48,128]{3,2,1,0:T(8,128)(2,1)S(1)}, u32[]{:S(2)}, u32[]{:S(2)}) %collective-permute-start.4) | collective-permute-done | bytes 36896 | tf_op jit(solution)/shard_map/ppermute | solution.py:293
  67.2 1.9 %collective-permute-start.7 = (bf16[3,3,48,128]{3,2,1,0:T(8,128)(2,1)S(1)}, bf16[3,3,48,128]{3,2,1,0:T(8,128)(2,1)S(1)}, u32[]{:S(2)}, u32[]{:S(2)}) collective-permute-start(bf16[3,3,48,128]{3,2,1,0:T(8,128)(2,1)S(1)} %pad_maximum_fusion), channel_id=1, source_target_pairs={{0,16},{16,0},{32,48},{48,32},{64,80},{80,64},{96,112},{112,96},{1... | collective-permute-start | bytes 331784 | tf_op jit(solution)/shard_map/ppermute | solution.py:293
  69.2 4.6 %collective-permute-start.6 = (bf16[3,3,48,128]{3,2,1,0:T(8,128)(2,1)S(1)}, bf16[3,3,48,128]{3,2,1,0:T(8,128)(2,1)S(1)}, u32[]{:S(2)}, u32[]{:S(2)}) collective-permute-start(bf16[3,3,48,128]{3,2,1,0:T(8,128)(2,1)S(1)} %pad_maximum_fusion), channel_id=1, source_target_pairs={{0,240},{16,32},{32,16},{48,64},{64,48},{80,96},{96,80},{112,128},... | collective-permute-start | bytes 331784 | tf_op jit(solution)/shard_map/ppermute | solution.py:293
  73.7 0.0 collective-permute-done.7
  73.7 2.1 %collective-permute-done.6 = bf16[3,3,48,128]{3,2,1,0:T(8,128)(2,1)S(1)} collective-permute-done((bf16[3,3,48,128]{3,2,1,0:T(8,128)(2,1)S(1)}, bf16[3,3,48,128]{3,2,1,0:T(8,128)(2,1)S(1)}, u32[]{:S(2)}, u32[]{:S(2)}) %collective-permute-start.6) | collective-permute-done | bytes 110624 | tf_op jit(solution)/shard_map/ppermute | solution.py:293
  75.9 1.6 %second_layer.1 = (f32[1,48]{1,0:T(1,128)}, f32[1,128]{1,0:T(1,128)S(1)}) custom-call(bf16[768,1536]{1,0:T(8,128)(2,1)S(1)} %get-tuple-element.17.edges, bf16[432,128]{1,0:T(8,128)(2,1)S(1)} %bitcast.19, bf16[432,128]{1,0:T(8,128)(2,1)S(1)} %bitcast.17, bf16[432,128]{1,0:T(8,128)(2,1)S(1)} %bitcast.18, f32[2,16,128]{2,1,0:T(8,128)S(1)} %get-tuple-element.15.radial, ...), custom_call_target="tpu_custom_call" | custom-call | tf_op jit(solution)/shard_map/second_layer/pallas_call | solution.py:276
  77.5 17.3 %all_to_all.16 = f32[64,1,128]{2,1,0:T(1,128)S(1)} all-to-all(f32[64,1,128]{2,1,0:T(1,128)S(1)} %broadcast_in_dim.19), channel_id=1, replica_groups=mesh['gx'=4,'gy'=16,'gz'=16] {'gx','gz'}, dimensions={0} | all-to-all | bytes 65536 | tf_op jit(solution)/shard_map/all_to_all | solution.py:305
  94.9 17.2 %all_to_all.17 = f32[16,1,128]{2,1,0:T(1,128)S(1)} all-to-all(f32[16,1,128]{2,1,0:T(1,128)S(1)} %broadcast_in_dim.20), channel_id=1, replica_groups=mesh['gx'=4,'gy'=16,'gz'=16] {'gy'}, dimensions={0} | all-to-all | bytes 16384 | tf_op jit(solution)/shard_map/all_to_all | solution.py:305
  112.1 0.5 reduce_sum.21
  (5 shorter events, 0.1 us)
Async XLA Ops:
  28.8 16.1 %collective-permute-start.1 = (f32[9,4,48]{2,1,0:T(4,128)S(1)}, f32[9,4,48]{2,1,0:T(4,128)S(1)}, u32[]{:S(2)}, u32[]{:S(2)}) collective-permute-start(f32[9,4,48]{2,1,0:T(4,128)S(1)} %pick_records.1.middle), channel_id=1, source_target_pairs={{0,16},{16,0},{32,48},{48,32},{64,80},{80,64},{96,112},{112,96},{1... | collective-permute-start | bytes 20744 | tf_op jit(solution)/shard_map/ppermute | solution.py:293
  30.7 14.2 %collective-permute-start = (f32[9,4,48]{2,1,0:T(4,128)S(1)}, f32[9,4,48]{2,1,0:T(4,128)S(1)}, u32[]{:S(2)}, u32[]{:S(2)}) collective-permute-start(f32[9,4,48]{2,1,0:T(4,128)S(1)} %pick_records.1.middle), channel_id=1, source_target_pairs={{0,240},{16,32},{32,16},{48,64},{64,48},{80,96},{96,80},{112,128},... | collective-permute-start | bytes 20744 | tf_op jit(solution)/shard_map/ppermute | solution.py:293
  46.5 5.2 %collective-permute-start.3 = (bf16[1,48,128]{2,1,0:T(8,128)(2,1)S(1)}, bf16[1,48,128]{2,1,0:T(8,128)(2,1)S(1)}, u32[]{:S(2)}, u32[]{:S(2)}) collective-permute-start(bf16[1,48,128]{2,1,0:T(8,128)(2,1)S(1)} %get-tuple-element.18), channel_id=1, source_target_pairs={{0,1},{1,0},{2,3},{3,2},{4,5},{5,4},{6,7},{7,6},{8,9},{9,8},{10,11... | collective-permute-start | bytes 36872 | tf_op jit(solution)/shard_map/ppermute | solution.py:293
  49.4 8.9 %collective-permute-start.2 = (bf16[1,48,128]{2,1,0:T(8,128)(2,1)S(1)}, bf16[1,48,128]{2,1,0:T(8,128)(2,1)S(1)}, u32[]{:S(2)}, u32[]{:S(2)}) collective-permute-start(bf16[1,48,128]{2,1,0:T(8,128)(2,1)S(1)} %get-tuple-element.18), channel_id=1, source_target_pairs={{0,15},{1,2},{2,1},{3,4},{4,3},{5,6},{6,5},{7,8},{8,7},{9,10},{10,... | collective-permute-start | bytes 36872 | tf_op jit(solution)/shard_map/ppermute | solution.py:293
  58.3 5.6 %collective-permute-start.5 = (bf16[1,3,48,128]{3,2,1,0:T(8,128)(2,1)S(1)}, bf16[1,3,48,128]{3,2,1,0:T(8,128)(2,1)S(1)}, u32[]{:S(2)}, u32[]{:S(2)}) collective-permute-start(bf16[1,3,48,128]{3,2,1,0:T(8,128)(2,1)S(1)} %maximum_bitcast_fusion), channel_id=1, source_target_pairs={{0,256},{256,0},{512,768},{768,512},{1,257},{257,1},{513,769},{769... | collective-permute-start | bytes 110600 | tf_op jit(solution)/shard_map/ppermute | solution.py:293
  60.7 6.5 %collective-permute-start.4 = (bf16[1,3,48,128]{3,2,1,0:T(8,128)(2,1)S(1)}, bf16[1,3,48,128]{3,2,1,0:T(8,128)(2,1)S(1)}, u32[]{:S(2)}, u32[]{:S(2)}) collective-permute-start(bf16[1,3,48,128]{3,2,1,0:T(8,128)(2,1)S(1)} %maximum_bitcast_fusion), channel_id=1, source_target_pairs={{0,768},{256,512},{512,256},{768,0},{1,769},{257,513},{513,257},{7... | collective-permute-start | bytes 110600 | tf_op jit(solution)/shard_map/ppermute | solution.py:293
  67.2 6.5 %collective-permute-start.7 = (bf16[3,3,48,128]{3,2,1,0:T(8,128)(2,1)S(1)}, bf16[3,3,48,128]{3,2,1,0:T(8,128)(2,1)S(1)}, u32[]{:S(2)}, u32[]{:S(2)}) collective-permute-start(bf16[3,3,48,128]{3,2,1,0:T(8,128)(2,1)S(1)} %pad_maximum_fusion), channel_id=1, source_target_pairs={{0,16},{16,0},{32,48},{48,32},{64,80},{80,64},{96,112},{112,96},{1... | collective-permute-start | bytes 331784 | tf_op jit(solution)/shard_map/ppermute | solution.py:293
  69.2 6.7 %collective-permute-start.6 = (bf16[3,3,48,128]{3,2,1,0:T(8,128)(2,1)S(1)}, bf16[3,3,48,128]{3,2,1,0:T(8,128)(2,1)S(1)}, u32[]{:S(2)}, u32[]{:S(2)}) collective-permute-start(bf16[3,3,48,128]{3,2,1,0:T(8,128)(2,1)S(1)} %pad_maximum_fusion), channel_id=1, source_target_pairs={{0,240},{16,32},{32,16},{48,64},{64,48},{80,96},{96,80},{112,128},... | collective-permute-start | bytes 331784 | tf_op jit(solution)/shard_map/ppermute | solution.py:293

commit v3 on v2

--- a/solution.py
+++ b/solution.py
@@ -22,7 +22,7 @@
 
 
 def side(axis):
-    return 1 - 2 * (lax.axis_index(axis) & 1)
+    return 2 * (lax.axis_index(axis) & 1) - 1
 
 
 def kept(array):
@@ -290,7 +290,7 @@
     count = lax.axis_size(axis)
     near = [(i, i ^ 1) for i in range(count)]
     far = [(i, (i - 1 + 2 * (i & 1)) % count) for i in range(count)]
-    return lax.ppermute(block, axis, far), block, lax.ppermute(block, axis, near)
+    return lax.ppermute(block, axis, near), block, lax.ppermute(block, axis, far)
 
 
 def halo(block):

time: 113 us -> 110 us (0.973)
  waiting for transfers between devices: 12 us -> 9.27 us
  starting transfers between devices: 31.4 us -> 29 us
  blocking collectives: 61.8 us -> 64 us
    ppermute x4, waiting for transfers between devices: 12 us -> 6.95 us  [both_sides(): lax.ppermute(block, axis, far)]
    ppermute x4, waiting for transfers between devices: 0.01 us -> 2.32 us  [both_sides(): lax.ppermute(block, axis, near)]
    all_to_all x2, blocking collectives: 34.5 us -> 36.7 us  [summed(): row = jnp.sum(lax.all_to_all(copies, axes, 0, 0), axis=0)]
    ppermute x4, starting transfers between devices: 22.3 us -> 20.8 us  [both_sides(): lax.ppermute(block, axis, far)]
  transfers between devices with their start and end apart: 8 -> 8, of which waited for: 3 -> 6; matrix products, arithmetic and copies ran while one was open for 0% -> 0% of each run, Pallas kernels for 2% -> 2%
where the time goes in v3:
time: 110 us
  blocking collectives  64 us (58%)
  starting transfers between devices  29 us (26%)
  waiting for transfers between devices  9.27 us (8%)
  Pallas kernels  6.06 us (6%)
    all_to_all x2, blocking collectives, summed(): row = jnp.sum(lax.all_to_all(copies, axes, 0, 0), axis=0)  36.7 us
    all_to_all x1, blocking collectives, body(): records = picked(lax.all_to_all(records, ('gx', 'gz'), 0, 0))  27.3 us
    ppermute x4, starting transfers between devices, both_sides(): lax.ppermute(block, axis, far)  20.8 us
    ppermute x4, starting transfers between devices, both_sides(): lax.ppermute(block, axis, near)  8.15 us
    ppermute x4, waiting for transfers between devices, both_sides(): lax.ppermute(block, axis, far)  6.95 us
    ppermute x4, waiting for transfers between devices, both_sides(): lax.ppermute(block, axis, near)  2.32 us
  transfers between devices with their start and end apart: 8, of which 6 were waited for; matrix products, arithmetic and copies ran while one was open for 0% of the time, Pallas kernels for 2%

profile of v3, /device:TPU:1, one launch (start us, length us, event | category | flops | bytes accessed | tf_op | source)
XLA Modules:
  0.0 109.7 jit_solution(6051287011560529924)
XLA Ops:
  0.6 0.8 pack_records.1
  1.4 27.3 %all_to_all.15.records = f32[64,1,192]{2,1,0:T(1,128)S(1)} all-to-all(f32[64,1,192]{2,1,0:T(1,128)S(1)} %pack_records.1), channel_id=1, replica_groups=mesh['gx'=4,'gy'=16,'gz'=16] {'gx','gz'}, dimensions={0} | all-to-all | bytes 98304 | tf_op jit(solution)/shard_map/all_to_all | solution.py:323
  28.7 0.1 pick_records.1.middle
  28.8 11.9 %collective-permute-start.1 = (f32[9,4,48]{2,1,0:T(4,128)S(1)}, f32[9,4,48]{2,1,0:T(4,128)S(1)}, u32[]{:S(2)}, u32[]{:S(2)}) collective-permute-start(f32[9,4,48]{2,1,0:T(4,128)S(1)} %pick_records.1.middle), channel_id=1, source_target_pairs={{0,240},{16,32},{32,16},{48,64},{64,48},{80,96},{96,80},{112,128},... | collective-permute-start | bytes 20744 | tf_op jit(solution)/shard_map/ppermute | solution.py:293
  40.8 1.9 %collective-permute-start = (f32[9,4,48]{2,1,0:T(4,128)S(1)}, f32[9,4,48]{2,1,0:T(4,128)S(1)}, u32[]{:S(2)}, u32[]{:S(2)}) collective-permute-start(f32[9,4,48]{2,1,0:T(4,128)S(1)} %pick_records.1.middle), channel_id=1, source_target_pairs={{0,16},{16,0},{32,48},{48,32},{64,80},{80,64},{96,112},{112,96},{1... | collective-permute-start | bytes 20744 | tf_op jit(solution)/shard_map/ppermute | solution.py:293
  42.7 2.0 %prepare.1 = (bf16[48,1536]{1,0:T(8,128)(2,1)S(1)}, f32[16,512]{1,0:T(8,128)S(1)}, f32[2,16,128]{2,1,0:T(8,128)S(1)}, bf16[2,128,128]{2,1,0:T(8,128)(2,1)S(1)}, ...) custom-call(s32[48,128]{1,0:T(8,128)} %bitcast.23, s32[48]{0:T(128)} %bitcast.27, s32[1,48]{1,0:T(1,128)} %bitcast.25, ...), custom_call_target="tpu_custom_call" | custom-call | tf_op jit(solution)/shard_map/prepare/pallas_call | solution.py:167
  44.7 0.0 collective-permute-done.1.after
  44.7 0.6 collective-permute-done.before
  45.3 1.5 %first_layer.1 = (bf16[768,1536]{1,0:T(8,128)(2,1)S(1)}, bf16[1,48,128]{2,1,0:T(8,128)(2,1)S(1)}) custom-call(f32[9,4,48]{2,1,0:T(4,128)S(1)} %collective-permute-done.before, f32[9,4,48]{2,1,0:T(4,128)S(1)} %pick_records.1.middle, f32[9,4,48]{2,1,0:T(4,128)S(1)} %collective-permute-done.1.after, bf16[48,1536]{1,0:T(8,128)(2,1)S(1)} %get-tuple-element.12.counts, ...), custom_call_target="tpu_custom_call" | custom-call | tf_op jit(solution)/shard_map/first_layer/pallas_call | solution.py:252
  46.8 4.2 %collective-permute-start.3 = (bf16[1,48,128]{2,1,0:T(8,128)(2,1)S(1)}, bf16[1,48,128]{2,1,0:T(8,128)(2,1)S(1)}, u32[]{:S(2)}, u32[]{:S(2)}) collective-permute-start(bf16[1,48,128]{2,1,0:T(8,128)(2,1)S(1)} %get-tuple-element.18), channel_id=1, source_target_pairs={{0,15},{1,2},{2,1},{3,4},{4,3},{5,6},{6,5},{7,8},{8,7},{9,10},{10,... | collective-permute-start | bytes 36872 | tf_op jit(solution)/shard_map/ppermute | solution.py:293
  51.0 1.9 %collective-permute-start.2 = (bf16[1,48,128]{2,1,0:T(8,128)(2,1)S(1)}, bf16[1,48,128]{2,1,0:T(8,128)(2,1)S(1)}, u32[]{:S(2)}, u32[]{:S(2)}) collective-permute-start(bf16[1,48,128]{2,1,0:T(8,128)(2,1)S(1)} %get-tuple-element.18), channel_id=1, source_target_pairs={{0,1},{1,0},{2,3},{3,2},{4,5},{5,4},{6,7},{7,6},{8,9},{9,8},{10,11... | collective-permute-start | bytes 36872 | tf_op jit(solution)/shard_map/ppermute | solution.py:293
  52.9 2.8 %collective-permute-done.3 = bf16[1,48,128]{2,1,0:T(8,128)(2,1)S(1)} collective-permute-done((bf16[1,48,128]{2,1,0:T(8,128)(2,1)S(1)}, bf16[1,48,128]{2,1,0:T(8,128)(2,1)S(1)}, u32[]{:S(2)}, u32[]{:S(2)}) %collective-permute-start.3) | collective-permute-done | bytes 12320 | tf_op jit(solution)/shard_map/ppermute | solution.py:293
  55.7 0.0 collective-permute-done.2
  55.7 2.8 %collective-permute-start.5 = (bf16[1,3,48,128]{3,2,1,0:T(8,128)(2,1)S(1)}, bf16[1,3,48,128]{3,2,1,0:T(8,128)(2,1)S(1)}, u32[]{:S(2)}, u32[]{:S(2)}) collective-permute-start(bf16[1,3,48,128]{3,2,1,0:T(8,128)(2,1)S(1)} %maximum_bitcast_fusion), channel_id=1, source_target_pairs={{0,768},{256,512},{512,256},{768,0},{1,769},{257,513},{513,257},{7... | collective-permute-start | bytes 110600 | tf_op jit(solution)/shard_map/ppermute | solution.py:293
  58.6 1.9 %collective-permute-start.4 = (bf16[1,3,48,128]{3,2,1,0:T(8,128)(2,1)S(1)}, bf16[1,3,48,128]{3,2,1,0:T(8,128)(2,1)S(1)}, u32[]{:S(2)}, u32[]{:S(2)}) collective-permute-start(bf16[1,3,48,128]{3,2,1,0:T(8,128)(2,1)S(1)} %maximum_bitcast_fusion), channel_id=1, source_target_pairs={{0,256},{256,0},{512,768},{768,512},{1,257},{257,1},{513,769},{769... | collective-permute-start | bytes 110600 | tf_op jit(solution)/shard_map/ppermute | solution.py:293
  60.5 1.7 %collective-permute-done.5 = bf16[1,3,48,128]{3,2,1,0:T(8,128)(2,1)S(1)} collective-permute-done((bf16[1,3,48,128]{3,2,1,0:T(8,128)(2,1)S(1)}, bf16[1,3,48,128]{3,2,1,0:T(8,128)(2,1)S(1)}, u32[]{:S(2)}, u32[]{:S(2)}) %collective-permute-start.5) | collective-permute-done | bytes 36896 | tf_op jit(solution)/shard_map/ppermute | solution.py:293
  62.2 1.0 collective-permute-done.4
  63.3 1.9 %collective-permute-start.7 = (bf16[3,3,48,128]{3,2,1,0:T(8,128)(2,1)S(1)}, bf16[3,3,48,128]{3,2,1,0:T(8,128)(2,1)S(1)}, u32[]{:S(2)}, u32[]{:S(2)}) collective-permute-start(bf16[3,3,48,128]{3,2,1,0:T(8,128)(2,1)S(1)} %pad_maximum_fusion), channel_id=1, source_target_pairs={{0,240},{16,32},{32,16},{48,64},{64,48},{80,96},{96,80},{112,128},... | collective-permute-start | bytes 331784 | tf_op jit(solution)/shard_map/ppermute | solution.py:293
  65.2 2.4 %collective-permute-start.6 = (bf16[3,3,48,128]{3,2,1,0:T(8,128)(2,1)S(1)}, bf16[3,3,48,128]{3,2,1,0:T(8,128)(2,1)S(1)}, u32[]{:S(2)}, u32[]{:S(2)}) collective-permute-start(bf16[3,3,48,128]{3,2,1,0:T(8,128)(2,1)S(1)} %pad_maximum_fusion), channel_id=1, source_target_pairs={{0,16},{16,0},{32,48},{48,32},{64,80},{80,64},{96,112},{112,96},{1... | collective-permute-start | bytes 331784 | tf_op jit(solution)/shard_map/ppermute | solution.py:293
  67.6 2.4 %collective-permute-done.7 = bf16[3,3,48,128]{3,2,1,0:T(8,128)(2,1)S(1)} collective-permute-done((bf16[3,3,48,128]{3,2,1,0:T(8,128)(2,1)S(1)}, bf16[3,3,48,128]{3,2,1,0:T(8,128)(2,1)S(1)}, u32[]{:S(2)}, u32[]{:S(2)}) %collective-permute-start.7) | collective-permute-done | bytes 110624 | tf_op jit(solution)/shard_map/ppermute | solution.py:293
  70.0 0.7 collective-permute-done.6
  70.7 1.6 %second_layer.1 = (f32[1,48]{1,0:T(1,128)}, f32[1,128]{1,0:T(1,128)S(1)}) custom-call(bf16[768,1536]{1,0:T(8,128)(2,1)S(1)} %get-tuple-element.17.edges, bf16[432,128]{1,0:T(8,128)(2,1)S(1)} %bitcast.19, bf16[432,128]{1,0:T(8,128)(2,1)S(1)} %bitcast.17, bf16[432,128]{1,0:T(8,128)(2,1)S(1)} %bitcast.18, f32[2,16,128]{2,1,0:T(8,128)S(1)} %get-tuple-element.15.radial, ...), custom_call_target="tpu_custom_call" | custom-call | tf_op jit(solution)/shard_map/second_layer/pallas_call | solution.py:276
  72.4 20.1 %all_to_all.16 = f32[64,1,128]{2,1,0:T(1,128)S(1)} all-to-all(f32[64,1,128]{2,1,0:T(1,128)S(1)} %broadcast_in_dim.19), channel_id=1, replica_groups=mesh['gx'=4,'gy'=16,'gz'=16] {'gx','gz'}, dimensions={0} | all-to-all | bytes 65536 | tf_op jit(solution)/shard_map/all_to_all | solution.py:305
  92.5 16.6 %all_to_all.17 = f32[16,1,128]{2,1,0:T(1,128)S(1)} all-to-all(f32[16,1,128]{2,1,0:T(1,128)S(1)} %broadcast_in_dim.20), channel_id=1, replica_groups=mesh['gx'=4,'gy'=16,'gz'=16] {'gy'}, dimensions={0} | all-to-all | bytes 16384 | tf_op jit(solution)/shard_map/all_to_all | solution.py:305
  109.1 0.5 reduce_sum.21
  (5 shorter events, 0.1 us)
Async XLA Ops:
  28.8 15.9 %collective-permute-start.1 = (f32[9,4,48]{2,1,0:T(4,128)S(1)}, f32[9,4,48]{2,1,0:T(4,128)S(1)}, u32[]{:S(2)}, u32[]{:S(2)}) collective-permute-start(f32[9,4,48]{2,1,0:T(4,128)S(1)} %pick_records.1.middle), channel_id=1, source_target_pairs={{0,240},{16,32},{32,16},{48,64},{64,48},{80,96},{96,80},{112,128},... | collective-permute-start | bytes 20744 | tf_op jit(solution)/shard_map/ppermute | solution.py:293
  40.8 4.5 %collective-permute-start = (f32[9,4,48]{2,1,0:T(4,128)S(1)}, f32[9,4,48]{2,1,0:T(4,128)S(1)}, u32[]{:S(2)}, u32[]{:S(2)}) collective-permute-start(f32[9,4,48]{2,1,0:T(4,128)S(1)} %pick_records.1.middle), channel_id=1, source_target_pairs={{0,16},{16,0},{32,48},{48,32},{64,80},{80,64},{96,112},{112,96},{1... | collective-permute-start | bytes 20744 | tf_op jit(solution)/shard_map/ppermute | solution.py:293
  46.8 8.9 %collective-permute-start.3 = (bf16[1,48,128]{2,1,0:T(8,128)(2,1)S(1)}, bf16[1,48,128]{2,1,0:T(8,128)(2,1)S(1)}, u32[]{:S(2)}, u32[]{:S(2)}) collective-permute-start(bf16[1,48,128]{2,1,0:T(8,128)(2,1)S(1)} %get-tuple-element.18), channel_id=1, source_target_pairs={{0,15},{1,2},{2,1},{3,4},{4,3},{5,6},{6,5},{7,8},{8,7},{9,10},{10,... | collective-permute-start | bytes 36872 | tf_op jit(solution)/shard_map/ppermute | solution.py:293
  51.0 4.8 %collective-permute-start.2 = (bf16[1,48,128]{2,1,0:T(8,128)(2,1)S(1)}, bf16[1,48,128]{2,1,0:T(8,128)(2,1)S(1)}, u32[]{:S(2)}, u32[]{:S(2)}) collective-permute-start(bf16[1,48,128]{2,1,0:T(8,128)(2,1)S(1)} %get-tuple-element.18), channel_id=1, source_target_pairs={{0,1},{1,0},{2,3},{3,2},{4,5},{5,4},{6,7},{7,6},{8,9},{9,8},{10,11... | collective-permute-start | bytes 36872 | tf_op jit(solution)/shard_map/ppermute | solution.py:293
  55.7 6.5 %collective-permute-start.5 = (bf16[1,3,48,128]{3,2,1,0:T(8,128)(2,1)S(1)}, bf16[1,3,48,128]{3,2,1,0:T(8,128)(2,1)S(1)}, u32[]{:S(2)}, u32[]{:S(2)}) collective-permute-start(bf16[1,3,48,128]{3,2,1,0:T(8,128)(2,1)S(1)} %maximum_bitcast_fusion), channel_id=1, source_target_pairs={{0,768},{256,512},{512,256},{768,0},{1,769},{257,513},{513,257},{7... | collective-permute-start | bytes 110600 | tf_op jit(solution)/shard_map/ppermute | solution.py:293
  58.6 4.7 %collective-permute-start.4 = (bf16[1,3,48,128]{3,2,1,0:T(8,128)(2,1)S(1)}, bf16[1,3,48,128]{3,2,1,0:T(8,128)(2,1)S(1)}, u32[]{:S(2)}, u32[]{:S(2)}) collective-permute-start(bf16[1,3,48,128]{3,2,1,0:T(8,128)(2,1)S(1)} %maximum_bitcast_fusion), channel_id=1, source_target_pairs={{0,256},{256,0},{512,768},{768,512},{1,257},{257,1},{513,769},{769... | collective-permute-start | bytes 110600 | tf_op jit(solution)/shard_map/ppermute | solution.py:293
  63.3 6.7 %collective-permute-start.7 = (bf16[3,3,48,128]{3,2,1,0:T(8,128)(2,1)S(1)}, bf16[3,3,48,128]{3,2,1,0:T(8,128)(2,1)S(1)}, u32[]{:S(2)}, u32[]{:S(2)}) collective-permute-start(bf16[3,3,48,128]{3,2,1,0:T(8,128)(2,1)S(1)} %pad_maximum_fusion), channel_id=1, source_target_pairs={{0,240},{16,32},{32,16},{48,64},{64,48},{80,96},{96,80},{112,128},... | collective-permute-start | bytes 331784 | tf_op jit(solution)/shard_map/ppermute | solution.py:293
  65.2 5.5 %collective-permute-start.6 = (bf16[3,3,48,128]{3,2,1,0:T(8,128)(2,1)S(1)}, bf16[3,3,48,128]{3,2,1,0:T(8,128)(2,1)S(1)}, u32[]{:S(2)}, u32[]{:S(2)}) collective-permute-start(bf16[3,3,48,128]{3,2,1,0:T(8,128)(2,1)S(1)} %pad_maximum_fusion), channel_id=1, source_target_pairs={{0,16},{16,0},{32,48},{48,32},{64,80},{80,64},{96,112},{112,96},{1... | collective-permute-start | bytes 331784 | tf_op jit(solution)/shard_map/ppermute | solution.py:293

commit v4 on v3

--- a/solution.py
+++ b/solution.py
@@ -300,7 +300,7 @@
 
 
 def summed(row):
-    for axes in (("gx", "gz"), ("gy",)):
+    for axes in (("gy",), ("gx", "gz")):
         copies = jnp.broadcast_to(row[None], (lax.axis_size(axes),) + row.shape)
         row = jnp.sum(lax.all_to_all(copies, axes, 0, 0), axis=0)
     return row

time: 110 us -> 112 us (1.018)
  blocking collectives: 64 us -> 65.4 us
    all_to_all x2, blocking collectives: 36.7 us -> 38.1 us  [summed(): row = jnp.sum(lax.all_to_all(copies, axes, 0, 0), axis=0)]
where the time goes in v4:
time: 112 us; the launch traced here: 111 us
  blocking collectives  65.4 us (58%)
  starting transfers between devices  29 us (26%)
  waiting for transfers between devices  9.27 us (8%)
  Pallas kernels  6.06 us (5%)
    all_to_all x2, blocking collectives, summed(): row = jnp.sum(lax.all_to_all(copies, axes, 0, 0), axis=0)  38.1 us
    all_to_all x1, blocking collectives, body(): records = picked(lax.all_to_all(records, ('gx', 'gz'), 0, 0))  27.3 us
    ppermute x4, starting transfers between devices, both_sides(): lax.ppermute(block, axis, far)  20.8 us
    ppermute x4, starting transfers between devices, both_sides(): lax.ppermute(block, axis, near)  8.15 us
    ppermute x4, waiting for transfers between devices, both_sides(): lax.ppermute(block, axis, far)  6.95 us
    ppermute x4, waiting for transfers between devices, both_sides(): lax.ppermute(block, axis, near)  2.32 us
  transfers between devices with their start and end apart: 8, of which 6 were waited for; matrix products, arithmetic and copies ran while one was open for 0% of the time, Pallas kernels for 2%

profile of v4, /device:TPU:1, one launch (start us, length us, event | category | flops | bytes accessed | tf_op | source)
XLA Modules:
  0.0 111.1 jit_solution(5737642295982646741)
XLA Ops:
  0.6 0.8 pack_records.1
  1.4 27.3 %all_to_all.15.records = f32[64,1,192]{2,1,0:T(1,128)S(1)} all-to-all(f32[64,1,192]{2,1,0:T(1,128)S(1)} %pack_records.1), channel_id=1, replica_groups=mesh['gx'=4,'gy'=16,'gz'=16] {'gx','gz'}, dimensions={0} | all-to-all | bytes 98304 | tf_op jit(solution)/shard_map/all_to_all | solution.py:323
  28.7 0.1 pick_records.1.middle
  28.8 11.9 %collective-permute-start.1 = (f32[9,4,48]{2,1,0:T(4,128)S(1)}, f32[9,4,48]{2,1,0:T(4,128)S(1)}, u32[]{:S(2)}, u32[]{:S(2)}) collective-permute-start(f32[9,4,48]{2,1,0:T(4,128)S(1)} %pick_records.1.middle), channel_id=1, source_target_pairs={{0,240},{16,32},{32,16},{48,64},{64,48},{80,96},{96,80},{112,128},... | collective-permute-start | bytes 20744 | tf_op jit(solution)/shard_map/ppermute | solution.py:293
  40.8 1.9 %collective-permute-start = (f32[9,4,48]{2,1,0:T(4,128)S(1)}, f32[9,4,48]{2,1,0:T(4,128)S(1)}, u32[]{:S(2)}, u32[]{:S(2)}) collective-permute-start(f32[9,4,48]{2,1,0:T(4,128)S(1)} %pick_records.1.middle), channel_id=1, source_target_pairs={{0,16},{16,0},{32,48},{48,32},{64,80},{80,64},{96,112},{112,96},{1... | collective-permute-start | bytes 20744 | tf_op jit(solution)/shard_map/ppermute | solution.py:293
  42.7 2.0 %prepare.1 = (bf16[48,1536]{1,0:T(8,128)(2,1)S(1)}, f32[16,512]{1,0:T(8,128)S(1)}, f32[2,16,128]{2,1,0:T(8,128)S(1)}, bf16[2,128,128]{2,1,0:T(8,128)(2,1)S(1)}, ...) custom-call(s32[48,128]{1,0:T(8,128)} %bitcast.23, s32[48]{0:T(128)} %bitcast.27, s32[1,48]{1,0:T(1,128)} %bitcast.25, ...), custom_call_target="tpu_custom_call" | custom-call | tf_op jit(solution)/shard_map/prepare/pallas_call | solution.py:167
  44.7 0.0 collective-permute-done.1.after
  44.7 0.6 collective-permute-done.before
  45.3 1.5 %first_layer.1 = (bf16[768,1536]{1,0:T(8,128)(2,1)S(1)}, bf16[1,48,128]{2,1,0:T(8,128)(2,1)S(1)}) custom-call(f32[9,4,48]{2,1,0:T(4,128)S(1)} %collective-permute-done.before, f32[9,4,48]{2,1,0:T(4,128)S(1)} %pick_records.1.middle, f32[9,4,48]{2,1,0:T(4,128)S(1)} %collective-permute-done.1.after, bf16[48,1536]{1,0:T(8,128)(2,1)S(1)} %get-tuple-element.12.counts, ...), custom_call_target="tpu_custom_call" | custom-call | tf_op jit(solution)/shard_map/first_layer/pallas_call | solution.py:252
  46.8 4.2 %collective-permute-start.3 = (bf16[1,48,128]{2,1,0:T(8,128)(2,1)S(1)}, bf16[1,48,128]{2,1,0:T(8,128)(2,1)S(1)}, u32[]{:S(2)}, u32[]{:S(2)}) collective-permute-start(bf16[1,48,128]{2,1,0:T(8,128)(2,1)S(1)} %get-tuple-element.18), channel_id=1, source_target_pairs={{0,15},{1,2},{2,1},{3,4},{4,3},{5,6},{6,5},{7,8},{8,7},{9,10},{10,... | collective-permute-start | bytes 36872 | tf_op jit(solution)/shard_map/ppermute | solution.py:293
  51.0 1.9 %collective-permute-start.2 = (bf16[1,48,128]{2,1,0:T(8,128)(2,1)S(1)}, bf16[1,48,128]{2,1,0:T(8,128)(2,1)S(1)}, u32[]{:S(2)}, u32[]{:S(2)}) collective-permute-start(bf16[1,48,128]{2,1,0:T(8,128)(2,1)S(1)} %get-tuple-element.18), channel_id=1, source_target_pairs={{0,1},{1,0},{2,3},{3,2},{4,5},{5,4},{6,7},{7,6},{8,9},{9,8},{10,11... | collective-permute-start | bytes 36872 | tf_op jit(solution)/shard_map/ppermute | solution.py:293
  52.9 2.8 %collective-permute-done.3 = bf16[1,48,128]{2,1,0:T(8,128)(2,1)S(1)} collective-permute-done((bf16[1,48,128]{2,1,0:T(8,128)(2,1)S(1)}, bf16[1,48,128]{2,1,0:T(8,128)(2,1)S(1)}, u32[]{:S(2)}, u32[]{:S(2)}) %collective-permute-start.3) | collective-permute-done | bytes 12320 | tf_op jit(solution)/shard_map/ppermute | solution.py:293
  55.7 0.0 collective-permute-done.2
  55.7 2.8 %collective-permute-start.5 = (bf16[1,3,48,128]{3,2,1,0:T(8,128)(2,1)S(1)}, bf16[1,3,48,128]{3,2,1,0:T(8,128)(2,1)S(1)}, u32[]{:S(2)}, u32[]{:S(2)}) collective-permute-start(bf16[1,3,48,128]{3,2,1,0:T(8,128)(2,1)S(1)} %maximum_bitcast_fusion), channel_id=1, source_target_pairs={{0,768},{256,512},{512,256},{768,0},{1,769},{257,513},{513,257},{7... | collective-permute-start | bytes 110600 | tf_op jit(solution)/shard_map/ppermute | solution.py:293
  58.6 1.9 %collective-permute-start.4 = (bf16[1,3,48,128]{3,2,1,0:T(8,128)(2,1)S(1)}, bf16[1,3,48,128]{3,2,1,0:T(8,128)(2,1)S(1)}, u32[]{:S(2)}, u32[]{:S(2)}) collective-permute-start(bf16[1,3,48,128]{3,2,1,0:T(8,128)(2,1)S(1)} %maximum_bitcast_fusion), channel_id=1, source_target_pairs={{0,256},{256,0},{512,768},{768,512},{1,257},{257,1},{513,769},{769... | collective-permute-start | bytes 110600 | tf_op jit(solution)/shard_map/ppermute | solution.py:293
  60.5 1.7 %collective-permute-done.5 = bf16[1,3,48,128]{3,2,1,0:T(8,128)(2,1)S(1)} collective-permute-done((bf16[1,3,48,128]{3,2,1,0:T(8,128)(2,1)S(1)}, bf16[1,3,48,128]{3,2,1,0:T(8,128)(2,1)S(1)}, u32[]{:S(2)}, u32[]{:S(2)}) %collective-permute-start.5) | collective-permute-done | bytes 36896 | tf_op jit(solution)/shard_map/ppermute | solution.py:293
  62.2 1.0 collective-permute-done.4
  63.3 1.9 %collective-permute-start.7 = (bf16[3,3,48,128]{3,2,1,0:T(8,128)(2,1)S(1)}, bf16[3,3,48,128]{3,2,1,0:T(8,128)(2,1)S(1)}, u32[]{:S(2)}, u32[]{:S(2)}) collective-permute-start(bf16[3,3,48,128]{3,2,1,0:T(8,128)(2,1)S(1)} %pad_maximum_fusion), channel_id=1, source_target_pairs={{0,240},{16,32},{32,16},{48,64},{64,48},{80,96},{96,80},{112,128},... | collective-permute-start | bytes 331784 | tf_op jit(solution)/shard_map/ppermute | solution.py:293
  65.2 2.4 %collective-permute-start.6 = (bf16[3,3,48,128]{3,2,1,0:T(8,128)(2,1)S(1)}, bf16[3,3,48,128]{3,2,1,0:T(8,128)(2,1)S(1)}, u32[]{:S(2)}, u32[]{:S(2)}) collective-permute-start(bf16[3,3,48,128]{3,2,1,0:T(8,128)(2,1)S(1)} %pad_maximum_fusion), channel_id=1, source_target_pairs={{0,16},{16,0},{32,48},{48,32},{64,80},{80,64},{96,112},{112,96},{1... | collective-permute-start | bytes 331784 | tf_op jit(solution)/shard_map/ppermute | solution.py:293
  67.6 2.4 %collective-permute-done.7 = bf16[3,3,48,128]{3,2,1,0:T(8,128)(2,1)S(1)} collective-permute-done((bf16[3,3,48,128]{3,2,1,0:T(8,128)(2,1)S(1)}, bf16[3,3,48,128]{3,2,1,0:T(8,128)(2,1)S(1)}, u32[]{:S(2)}, u32[]{:S(2)}) %collective-permute-start.7) | collective-permute-done | bytes 110624 | tf_op jit(solution)/shard_map/ppermute | solution.py:293
  70.0 0.7 collective-permute-done.6
  70.7 1.6 %second_layer.1 = (f32[1,48]{1,0:T(1,128)}, f32[1,128]{1,0:T(1,128)S(1)}) custom-call(bf16[768,1536]{1,0:T(8,128)(2,1)S(1)} %get-tuple-element.17.edges, bf16[432,128]{1,0:T(8,128)(2,1)S(1)} %bitcast.19, bf16[432,128]{1,0:T(8,128)(2,1)S(1)} %bitcast.17, bf16[432,128]{1,0:T(8,128)(2,1)S(1)} %bitcast.18, f32[2,16,128]{2,1,0:T(8,128)S(1)} %get-tuple-element.15.radial, ...), custom_call_target="tpu_custom_call" | custom-call | tf_op jit(solution)/shard_map/second_layer/pallas_call | solution.py:276
  72.4 16.3 %all_to_all.16 = f32[16,1,128]{2,1,0:T(1,128)S(1)} all-to-all(f32[16,1,128]{2,1,0:T(1,128)S(1)} %broadcast_in_dim.19), channel_id=1, replica_groups=mesh['gx'=4,'gy'=16,'gz'=16] {'gy'}, dimensions={0} | all-to-all | bytes 16384 | tf_op jit(solution)/shard_map/all_to_all | solution.py:305
  88.7 21.8 %all_to_all.17 = f32[64,1,128]{2,1,0:T(1,128)S(1)} all-to-all(f32[64,1,128]{2,1,0:T(1,128)S(1)} %broadcast_in_dim.20), channel_id=1, replica_groups=mesh['gx'=4,'gy'=16,'gz'=16] {'gx','gz'}, dimensions={0} | all-to-all | bytes 65536 | tf_op jit(solution)/shard_map/all_to_all | solution.py:305
  110.5 0.5 reduce_sum.21
  (5 shorter events, 0.1 us)
Async XLA Ops:
  28.8 15.9 %collective-permute-start.1 = (f32[9,4,48]{2,1,0:T(4,128)S(1)}, f32[9,4,48]{2,1,0:T(4,128)S(1)}, u32[]{:S(2)}, u32[]{:S(2)}) collective-permute-start(f32[9,4,48]{2,1,0:T(4,128)S(1)} %pick_records.1.middle), channel_id=1, source_target_pairs={{0,240},{16,32},{32,16},{48,64},{64,48},{80,96},{96,80},{112,128},... | collective-permute-start | bytes 20744 | tf_op jit(solution)/shard_map/ppermute | solution.py:293
  40.8 4.5 %collective-permute-start = (f32[9,4,48]{2,1,0:T(4,128)S(1)}, f32[9,4,48]{2,1,0:T(4,128)S(1)}, u32[]{:S(2)}, u32[]{:S(2)}) collective-permute-start(f32[9,4,48]{2,1,0:T(4,128)S(1)} %pick_records.1.middle), channel_id=1, source_target_pairs={{0,16},{16,0},{32,48},{48,32},{64,80},{80,64},{96,112},{112,96},{1... | collective-permute-start | bytes 20744 | tf_op jit(solution)/shard_map/ppermute | solution.py:293
  46.8 8.9 %collective-permute-start.3 = (bf16[1,48,128]{2,1,0:T(8,128)(2,1)S(1)}, bf16[1,48,128]{2,1,0:T(8,128)(2,1)S(1)}, u32[]{:S(2)}, u32[]{:S(2)}) collective-permute-start(bf16[1,48,128]{2,1,0:T(8,128)(2,1)S(1)} %get-tuple-element.18), channel_id=1, source_target_pairs={{0,15},{1,2},{2,1},{3,4},{4,3},{5,6},{6,5},{7,8},{8,7},{9,10},{10,... | collective-permute-start | bytes 36872 | tf_op jit(solution)/shard_map/ppermute | solution.py:293
  51.0 4.8 %collective-permute-start.2 = (bf16[1,48,128]{2,1,0:T(8,128)(2,1)S(1)}, bf16[1,48,128]{2,1,0:T(8,128)(2,1)S(1)}, u32[]{:S(2)}, u32[]{:S(2)}) collective-permute-start(bf16[1,48,128]{2,1,0:T(8,128)(2,1)S(1)} %get-tuple-element.18), channel_id=1, source_target_pairs={{0,1},{1,0},{2,3},{3,2},{4,5},{5,4},{6,7},{7,6},{8,9},{9,8},{10,11... | collective-permute-start | bytes 36872 | tf_op jit(solution)/shard_map/ppermute | solution.py:293
  55.7 6.5 %collective-permute-start.5 = (bf16[1,3,48,128]{3,2,1,0:T(8,128)(2,1)S(1)}, bf16[1,3,48,128]{3,2,1,0:T(8,128)(2,1)S(1)}, u32[]{:S(2)}, u32[]{:S(2)}) collective-permute-start(bf16[1,3,48,128]{3,2,1,0:T(8,128)(2,1)S(1)} %maximum_bitcast_fusion), channel_id=1, source_target_pairs={{0,768},{256,512},{512,256},{768,0},{1,769},{257,513},{513,257},{7... | collective-permute-start | bytes 110600 | tf_op jit(solution)/shard_map/ppermute | solution.py:293
  58.6 4.7 %collective-permute-start.4 = (bf16[1,3,48,128]{3,2,1,0:T(8,128)(2,1)S(1)}, bf16[1,3,48,128]{3,2,1,0:T(8,128)(2,1)S(1)}, u32[]{:S(2)}, u32[]{:S(2)}) collective-permute-start(bf16[1,3,48,128]{3,2,1,0:T(8,128)(2,1)S(1)} %maximum_bitcast_fusion), channel_id=1, source_target_pairs={{0,256},{256,0},{512,768},{768,512},{1,257},{257,1},{513,769},{769... | collective-permute-start | bytes 110600 | tf_op jit(solution)/shard_map/ppermute | solution.py:293
  63.3 6.7 %collective-permute-start.7 = (bf16[3,3,48,128]{3,2,1,0:T(8,128)(2,1)S(1)}, bf16[3,3,48,128]{3,2,1,0:T(8,128)(2,1)S(1)}, u32[]{:S(2)}, u32[]{:S(2)}) collective-permute-start(bf16[3,3,48,128]{3,2,1,0:T(8,128)(2,1)S(1)} %pad_maximum_fusion), channel_id=1, source_target_pairs={{0,240},{16,32},{32,16},{48,64},{64,48},{80,96},{96,80},{112,128},... | collective-permute-start | bytes 331784 | tf_op jit(solution)/shard_map/ppermute | solution.py:293
  65.2 5.5 %collective-permute-start.6 = (bf16[3,3,48,128]{3,2,1,0:T(8,128)(2,1)S(1)}, bf16[3,3,48,128]{3,2,1,0:T(8,128)(2,1)S(1)}, u32[]{:S(2)}, u32[]{:S(2)}) collective-permute-start(bf16[3,3,48,128]{3,2,1,0:T(8,128)(2,1)S(1)} %pad_maximum_fusion), channel_id=1, source_target_pairs={{0,16},{16,0},{32,48},{48,32},{64,80},{80,64},{96,112},{112,96},{1... | collective-permute-start | bytes 331784 | tf_op jit(solution)/shard_map/ppermute | solution.py:293

commit v5 on v3

--- a/solution.py
+++ b/solution.py
@@ -76,7 +76,7 @@
         for k in range(3):
             record = records[row * NZ + ((z + (k - 1) * side("gz")) & (NZ - 1))]
             for d in range(4):
-                out[i * 3 + k, d : d + 1] = record[:, d * SLOTS : (d + 1) * SLOTS]
+                out[k * 3 + i, d : d + 1] = record[:, d * SLOTS : (d + 1) * SLOTS]
 
 
 def picked(records):
@@ -132,7 +132,7 @@
     x = 1 + (depth - 1) * side("gx")
     y = 1 + (across - depth * 3 - 1) * side("gy")
     z = 1 + (offset - across * 3 - 1) * side("gz")
-    place = y * LANES + (x * 3 + z) * SLOTS + slot
+    place = y * LANES + (z * 3 + x) * SLOTS + slot
     high[...] = place >> 7
     low[...] = place & 127
     lane = lax.broadcasted_iota(jnp.int32, (1, NB), 1)
@@ -221,8 +221,8 @@
     kind_of = lax.broadcasted_iota(jnp.int32, (8, LANES), 0).astype(jnp.float32)
     cell = lax.broadcasted_iota(jnp.int32, (4, LANES), 1) // SLOTS
     part_of = lax.broadcasted_iota(jnp.int32, (4, LANES), 0)
-    across = (cell // 3 - 1) * side("gx")
-    along = (cell % 3 - 1) * side("gz")
+    across = (cell % 3 - 1) * side("gx")
+    along = (cell // 3 - 1) * side("gz")
     centre = jnp.transpose(middle[4])
     tables = []
     for y, records in enumerate((before, middle, after)):
@@ -294,8 +294,8 @@
 
 
 def halo(block):
-    line = jnp.concatenate(both_sides(block, "gz"), axis=0)
-    sheet = jnp.concatenate(both_sides(line[None], "gx"), axis=0)
+    line = jnp.concatenate(both_sides(block, "gx"), axis=0)
+    sheet = jnp.concatenate(both_sides(line[None], "gz"), axis=0)
     return both_sides(sheet, "gy")
 
 

time: 110 us -> 110 us (level)
  starting transfers between devices: 29 us -> 31.7 us
  waiting for transfers between devices: 9.27 us -> 7.7 us
  blocking collectives: 64 us -> 62.8 us
    ppermute x4, starting transfers between devices: 20.8 us -> 23.9 us  [both_sides(): lax.ppermute(block, axis, far)]
    ppermute x4, waiting for transfers between devices: 6.95 us -> 4.64 us  [both_sides(): lax.ppermute(block, axis, far)]
    all_to_all x2, blocking collectives: 36.7 us -> 35.5 us  [summed(): row = jnp.sum(lax.all_to_all(copies, axes, 0, 0), axis=0)]
where the time goes in v5:
time: 110 us
  blocking collectives  62.8 us (57%)
  starting transfers between devices  31.7 us (29%)
  waiting for transfers between devices  7.7 us (7%)
  Pallas kernels  6.06 us (6%)
    all_to_all x2, blocking collectives, summed(): row = jnp.sum(lax.all_to_all(copies, axes, 0, 0), axis=0)  35.5 us
    all_to_all x1, blocking collectives, body(): records = picked(lax.all_to_all(records, ('gx', 'gz'), 0, 0))  27.3 us
    ppermute x4, starting transfers between devices, both_sides(): lax.ppermute(block, axis, far)  23.9 us
    ppermute x4, starting transfers between devices, both_sides(): lax.ppermute(block, axis, near)  7.8 us
    ppermute x4, waiting for transfers between devices, both_sides(): lax.ppermute(block, axis, far)  4.64 us
    ppermute x4, waiting for transfers between devices, both_sides(): lax.ppermute(block, axis, near)  3.06 us
  transfers between devices with their start and end apart: 8, of which 6 were waited for; matrix products, arithmetic and copies ran while one was open for 0% of the time, Pallas kernels for 2%

profile of v5, /device:TPU:1, one launch (start us, length us, event | category | flops | bytes accessed | tf_op | source)
XLA Modules:
  0.0 109.6 jit_solution(4635114274216490326)
XLA Ops:
  0.6 0.8 pack_records.1
  1.4 27.3 %all_to_all.15.records = f32[64,1,192]{2,1,0:T(1,128)S(1)} all-to-all(f32[64,1,192]{2,1,0:T(1,128)S(1)} %pack_records.1), channel_id=1, replica_groups=mesh['gx'=4,'gy'=16,'gz'=16] {'gx','gz'}, dimensions={0} | all-to-all | bytes 98304 | tf_op jit(solution)/shard_map/all_to_all | solution.py:323
  28.7 0.1 pick_records.1.middle
  28.8 11.9 %collective-permute-start.1 = (f32[9,4,48]{2,1,0:T(4,128)S(1)}, f32[9,4,48]{2,1,0:T(4,128)S(1)}, u32[]{:S(2)}, u32[]{:S(2)}) collective-permute-start(f32[9,4,48]{2,1,0:T(4,128)S(1)} %pick_records.1.middle), channel_id=1, source_target_pairs={{0,240},{16,32},{32,16},{48,64},{64,48},{80,96},{96,80},{112,128},... | collective-permute-start | bytes 20744 | tf_op jit(solution)/shard_map/ppermute | solution.py:293
  40.8 1.9 %collective-permute-start = (f32[9,4,48]{2,1,0:T(4,128)S(1)}, f32[9,4,48]{2,1,0:T(4,128)S(1)}, u32[]{:S(2)}, u32[]{:S(2)}) collective-permute-start(f32[9,4,48]{2,1,0:T(4,128)S(1)} %pick_records.1.middle), channel_id=1, source_target_pairs={{0,16},{16,0},{32,48},{48,32},{64,80},{80,64},{96,112},{112,96},{1... | collective-permute-start | bytes 20744 | tf_op jit(solution)/shard_map/ppermute | solution.py:293
  42.7 2.0 %prepare.1 = (bf16[48,1536]{1,0:T(8,128)(2,1)S(1)}, f32[16,512]{1,0:T(8,128)S(1)}, f32[2,16,128]{2,1,0:T(8,128)S(1)}, bf16[2,128,128]{2,1,0:T(8,128)(2,1)S(1)}, ...) custom-call(s32[48,128]{1,0:T(8,128)} %bitcast.23, s32[48]{0:T(128)} %bitcast.27, s32[1,48]{1,0:T(1,128)} %bitcast.25, ...), custom_call_target="tpu_custom_call" | custom-call | tf_op jit(solution)/shard_map/prepare/pallas_call | solution.py:167
  44.7 0.0 collective-permute-done.1.after
  44.7 0.6 collective-permute-done.before
  45.3 1.5 %first_layer.1 = (bf16[768,1536]{1,0:T(8,128)(2,1)S(1)}, bf16[1,48,128]{2,1,0:T(8,128)(2,1)S(1)}) custom-call(f32[9,4,48]{2,1,0:T(4,128)S(1)} %collective-permute-done.before, f32[9,4,48]{2,1,0:T(4,128)S(1)} %pick_records.1.middle, f32[9,4,48]{2,1,0:T(4,128)S(1)} %collective-permute-done.1.after, bf16[48,1536]{1,0:T(8,128)(2,1)S(1)} %get-tuple-element.12.counts, ...), custom_call_target="tpu_custom_call" | custom-call | tf_op jit(solution)/shard_map/first_layer/pallas_call | solution.py:252
  46.8 2.4 %collective-permute-start.3 = (bf16[1,48,128]{2,1,0:T(8,128)(2,1)S(1)}, bf16[1,48,128]{2,1,0:T(8,128)(2,1)S(1)}, u32[]{:S(2)}, u32[]{:S(2)}) collective-permute-start(bf16[1,48,128]{2,1,0:T(8,128)(2,1)S(1)} %get-tuple-element.18), channel_id=1, source_target_pairs={{0,768},{256,512},{512,256},{768,0},{1,769},{257,513},{513,257},{7... | collective-permute-start | bytes 36872 | tf_op jit(solution)/shard_map/ppermute | solution.py:293
  49.2 2.0 %collective-permute-start.2 = (bf16[1,48,128]{2,1,0:T(8,128)(2,1)S(1)}, bf16[1,48,128]{2,1,0:T(8,128)(2,1)S(1)}, u32[]{:S(2)}, u32[]{:S(2)}) collective-permute-start(bf16[1,48,128]{2,1,0:T(8,128)(2,1)S(1)} %get-tuple-element.18), channel_id=1, source_target_pairs={{0,256},{256,0},{512,768},{768,512},{1,257},{257,1},{513,769},{769... | collective-permute-start | bytes 36872 | tf_op jit(solution)/shard_map/ppermute | solution.py:293
  51.2 1.8 %collective-permute-done.3 = bf16[1,48,128]{2,1,0:T(8,128)(2,1)S(1)} collective-permute-done((bf16[1,48,128]{2,1,0:T(8,128)(2,1)S(1)}, bf16[1,48,128]{2,1,0:T(8,128)(2,1)S(1)}, u32[]{:S(2)}, u32[]{:S(2)}) %collective-permute-start.3) | collective-permute-done | bytes 12320 | tf_op jit(solution)/shard_map/ppermute | solution.py:293
  53.0 0.6 collective-permute-done.2
  53.7 7.7 %collective-permute-start.5 = (bf16[1,3,48,128]{3,2,1,0:T(8,128)(2,1)S(1)}, bf16[1,3,48,128]{3,2,1,0:T(8,128)(2,1)S(1)}, u32[]{:S(2)}, u32[]{:S(2)}) collective-permute-start(bf16[1,3,48,128]{3,2,1,0:T(8,128)(2,1)S(1)} %maximum_bitcast_fusion), channel_id=1, source_target_pairs={{0,15},{1,2},{2,1},{3,4},{4,3},{5,6},{6,5},{7,8},{8,7},{9,10},{10,... | collective-permute-start | bytes 110600 | tf_op jit(solution)/shard_map/ppermute | solution.py:293
  61.4 1.9 %collective-permute-start.4 = (bf16[1,3,48,128]{3,2,1,0:T(8,128)(2,1)S(1)}, bf16[1,3,48,128]{3,2,1,0:T(8,128)(2,1)S(1)}, u32[]{:S(2)}, u32[]{:S(2)}) collective-permute-start(bf16[1,3,48,128]{3,2,1,0:T(8,128)(2,1)S(1)} %maximum_bitcast_fusion), channel_id=1, source_target_pairs={{0,1},{1,0},{2,3},{3,2},{4,5},{5,4},{6,7},{7,6},{8,9},{9,8},{10,11... | collective-permute-start | bytes 110600 | tf_op jit(solution)/shard_map/ppermute | solution.py:293
  63.3 0.0 collective-permute-done.5
  63.3 1.2 %collective-permute-done.4 = bf16[1,3,48,128]{3,2,1,0:T(8,128)(2,1)S(1)} collective-permute-done((bf16[1,3,48,128]{3,2,1,0:T(8,128)(2,1)S(1)}, bf16[1,3,48,128]{3,2,1,0:T(8,128)(2,1)S(1)}, u32[]{:S(2)}, u32[]{:S(2)}) %collective-permute-start.4) | collective-permute-done | bytes 36896 | tf_op jit(solution)/shard_map/ppermute | solution.py:293
  64.5 1.9 %collective-permute-start.7 = (bf16[3,3,48,128]{3,2,1,0:T(8,128)(2,1)S(1)}, bf16[3,3,48,128]{3,2,1,0:T(8,128)(2,1)S(1)}, u32[]{:S(2)}, u32[]{:S(2)}) collective-permute-start(bf16[3,3,48,128]{3,2,1,0:T(8,128)(2,1)S(1)} %pad_maximum_fusion), channel_id=1, source_target_pairs={{0,240},{16,32},{32,16},{48,64},{64,48},{80,96},{96,80},{112,128},... | collective-permute-start | bytes 331784 | tf_op jit(solution)/shard_map/ppermute | solution.py:293
  66.4 1.9 %collective-permute-start.6 = (bf16[3,3,48,128]{3,2,1,0:T(8,128)(2,1)S(1)}, bf16[3,3,48,128]{3,2,1,0:T(8,128)(2,1)S(1)}, u32[]{:S(2)}, u32[]{:S(2)}) collective-permute-start(bf16[3,3,48,128]{3,2,1,0:T(8,128)(2,1)S(1)} %pad_maximum_fusion), channel_id=1, source_target_pairs={{0,16},{16,0},{32,48},{48,32},{64,80},{80,64},{96,112},{112,96},{1... | collective-permute-start | bytes 331784 | tf_op jit(solution)/shard_map/ppermute | solution.py:293
  68.4 2.8 %collective-permute-done.7 = bf16[3,3,48,128]{3,2,1,0:T(8,128)(2,1)S(1)} collective-permute-done((bf16[3,3,48,128]{3,2,1,0:T(8,128)(2,1)S(1)}, bf16[3,3,48,128]{3,2,1,0:T(8,128)(2,1)S(1)}, u32[]{:S(2)}, u32[]{:S(2)}) %collective-permute-start.7) | collective-permute-done | bytes 110624 | tf_op jit(solution)/shard_map/ppermute | solution.py:293
  71.2 0.7 collective-permute-done.6
  71.9 1.6 %second_layer.1 = (f32[1,48]{1,0:T(1,128)}, f32[1,128]{1,0:T(1,128)S(1)}) custom-call(bf16[768,1536]{1,0:T(8,128)(2,1)S(1)} %get-tuple-element.17.edges, bf16[432,128]{1,0:T(8,128)(2,1)S(1)} %bitcast.19, bf16[432,128]{1,0:T(8,128)(2,1)S(1)} %bitcast.17, bf16[432,128]{1,0:T(8,128)(2,1)S(1)} %bitcast.18, f32[2,16,128]{2,1,0:T(8,128)S(1)} %get-tuple-element.15.radial, ...), custom_call_target="tpu_custom_call" | custom-call | tf_op jit(solution)/shard_map/second_layer/pallas_call | solution.py:276
  73.6 18.9 %all_to_all.16 = f32[64,1,128]{2,1,0:T(1,128)S(1)} all-to-all(f32[64,1,128]{2,1,0:T(1,128)S(1)} %broadcast_in_dim.19), channel_id=1, replica_groups=mesh['gx'=4,'gy'=16,'gz'=16] {'gx','gz'}, dimensions={0} | all-to-all | bytes 65536 | tf_op jit(solution)/shard_map/all_to_all | solution.py:305
  92.5 16.6 %all_to_all.17 = f32[16,1,128]{2,1,0:T(1,128)S(1)} all-to-all(f32[16,1,128]{2,1,0:T(1,128)S(1)} %broadcast_in_dim.20), channel_id=1, replica_groups=mesh['gx'=4,'gy'=16,'gz'=16] {'gy'}, dimensions={0} | all-to-all | bytes 16384 | tf_op jit(solution)/shard_map/all_to_all | solution.py:305
  109.1 0.5 reduce_sum.21
  (5 shorter events, 0.1 us)
Async XLA Ops:
  28.8 15.9 %collective-permute-start.1 = (f32[9,4,48]{2,1,0:T(4,128)S(1)}, f32[9,4,48]{2,1,0:T(4,128)S(1)}, u32[]{:S(2)}, u32[]{:S(2)}) collective-permute-start(f32[9,4,48]{2,1,0:T(4,128)S(1)} %pick_records.1.middle), channel_id=1, source_target_pairs={{0,240},{16,32},{32,16},{48,64},{64,48},{80,96},{96,80},{112,128},... | collective-permute-start | bytes 20744 | tf_op jit(solution)/shard_map/ppermute | solution.py:293
  40.8 4.5 %collective-permute-start = (f32[9,4,48]{2,1,0:T(4,128)S(1)}, f32[9,4,48]{2,1,0:T(4,128)S(1)}, u32[]{:S(2)}, u32[]{:S(2)}) collective-permute-start(f32[9,4,48]{2,1,0:T(4,128)S(1)} %pick_records.1.middle), channel_id=1, source_target_pairs={{0,16},{16,0},{32,48},{48,32},{64,80},{80,64},{96,112},{112,96},{1... | collective-permute-start | bytes 20744 | tf_op jit(solution)/shard_map/ppermute | solution.py:293
  46.8 6.2 %collective-permute-start.3 = (bf16[1,48,128]{2,1,0:T(8,128)(2,1)S(1)}, bf16[1,48,128]{2,1,0:T(8,128)(2,1)S(1)}, u32[]{:S(2)}, u32[]{:S(2)}) collective-permute-start(bf16[1,48,128]{2,1,0:T(8,128)(2,1)S(1)} %get-tuple-element.18), channel_id=1, source_target_pairs={{0,768},{256,512},{512,256},{768,0},{1,769},{257,513},{513,257},{7... | collective-permute-start | bytes 36872 | tf_op jit(solution)/shard_map/ppermute | solution.py:293
  49.2 4.4 %collective-permute-start.2 = (bf16[1,48,128]{2,1,0:T(8,128)(2,1)S(1)}, bf16[1,48,128]{2,1,0:T(8,128)(2,1)S(1)}, u32[]{:S(2)}, u32[]{:S(2)}) collective-permute-start(bf16[1,48,128]{2,1,0:T(8,128)(2,1)S(1)} %get-tuple-element.18), channel_id=1, source_target_pairs={{0,256},{256,0},{512,768},{768,512},{1,257},{257,1},{513,769},{769... | collective-permute-start | bytes 36872 | tf_op jit(solution)/shard_map/ppermute | solution.py:293
  53.7 9.6 %collective-permute-start.5 = (bf16[1,3,48,128]{3,2,1,0:T(8,128)(2,1)S(1)}, bf16[1,3,48,128]{3,2,1,0:T(8,128)(2,1)S(1)}, u32[]{:S(2)}, u32[]{:S(2)}) collective-permute-start(bf16[1,3,48,128]{3,2,1,0:T(8,128)(2,1)S(1)} %maximum_bitcast_fusion), channel_id=1, source_target_pairs={{0,15},{1,2},{2,1},{3,4},{4,3},{5,6},{6,5},{7,8},{8,7},{9,10},{10,... | collective-permute-start | bytes 110600 | tf_op jit(solution)/shard_map/ppermute | solution.py:293
  61.4 3.1 %collective-permute-start.4 = (bf16[1,3,48,128]{3,2,1,0:T(8,128)(2,1)S(1)}, bf16[1,3,48,128]{3,2,1,0:T(8,128)(2,1)S(1)}, u32[]{:S(2)}, u32[]{:S(2)}) collective-permute-start(bf16[1,3,48,128]{3,2,1,0:T(8,128)(2,1)S(1)} %maximum_bitcast_fusion), channel_id=1, source_target_pairs={{0,1},{1,0},{2,3},{3,2},{4,5},{5,4},{6,7},{7,6},{8,9},{9,8},{10,11... | collective-permute-start | bytes 110600 | tf_op jit(solution)/shard_map/ppermute | solution.py:293
  64.5 6.7 %collective-permute-start.7 = (bf16[3,3,48,128]{3,2,1,0:T(8,128)(2,1)S(1)}, bf16[3,3,48,128]{3,2,1,0:T(8,128)(2,1)S(1)}, u32[]{:S(2)}, u32[]{:S(2)}) collective-permute-start(bf16[3,3,48,128]{3,2,1,0:T(8,128)(2,1)S(1)} %pad_maximum_fusion), channel_id=1, source_target_pairs={{0,240},{16,32},{32,16},{48,64},{64,48},{80,96},{96,80},{112,128},... | collective-permute-start | bytes 331784 | tf_op jit(solution)/shard_map/ppermute | solution.py:293
  66.4 5.5 %collective-permute-start.6 = (bf16[3,3,48,128]{3,2,1,0:T(8,128)(2,1)S(1)}, bf16[3,3,48,128]{3,2,1,0:T(8,128)(2,1)S(1)}, u32[]{:S(2)}, u32[]{:S(2)}) collective-permute-start(bf16[3,3,48,128]{3,2,1,0:T(8,128)(2,1)S(1)} %pad_maximum_fusion), channel_id=1, source_target_pairs={{0,16},{16,0},{32,48},{48,32},{64,80},{80,64},{96,112},{112,96},{1... | collective-permute-start | bytes 331784 | tf_op jit(solution)/shard_map/ppermute | solution.py:293
